TPU v7x, 128 devices: a whole 4x4x4 slice. The times are simulated.
128 devices in a mesh: grp: 4 (over z), wave: 32 (over x, y, core).
Axes of the slice: x: 4, y: 4, z: 4, core: 2. Of those that a mesh axis runs over, the one named last changes fastest.
Arguments:
- state: bfloat16 [275, 984320], P(None, ('grp', 'wave')), may hold values from -6 to 6
- held_orders: int32 [640], P(('grp', 'wave')), may hold values from -1 to 383, as said below
- pair_lows: int32 [384], P(('grp', 'wave')), may hold values from 0 to 383, each once
- inverses: bfloat16 [384, 2, 137, 137], P(('grp', 'wave')), may hold values from -2 to 3
- height_operator: bfloat16 [137, 137], replicated, may hold values from -0.5 to 0.5
- pressure_column: bfloat16 [137], replicated, may hold values from -5 to 5
- thermal_response_matrix: bfloat16 [137, 137], replicated, may hold values from -0.5 to 0.5
- mass_row: bfloat16 [137], replicated, may hold values from -0.5 to 0.5
Outputs:
- advanced: bfloat16 [275, 984320], P(None, ('grp', 'wave'))
Inputs may be any that keep to these rules, and one draw needn't show every extreme that they name: `held_orders`: each of 0 to 383 appears exactly once, all other entries are -1; some device has all 5 of its slots filled.
All inputs are finite; a program needn't handle non-finite values.
Results may differ from a plain program's by a relative error of at most 0.0052.
Values may be sent and summed in bfloat16 or wider, within the bound.
A program may use at most 128 MiB of HBM per device.

v0:
```python
import jax
import jax.numpy as jnp
from jax import lax
from jax.sharding import Mesh
from jax.sharding import PartitionSpec as P

GRP_WAVE = ("grp", "wave_0", "wave_1", "wave_2")
WAVE = ("wave_0", "wave_1", "wave_2")


def in_order(tiles, dim):
    shape = list(tiles.shape[1:])
    shape[dim] *= tiles.shape[0]
    return jnp.moveaxis(tiles, 0, dim).reshape(shape)


def all_blocks(shard, axes, turns):
    tiles = shard[None]
    for k in turns:
        tiles = lax.all_gather(tiles, axes[k], axis=0, tiled=True)
    held = [lax.axis_size(axes[k]) for k in reversed(turns)]
    tiles = tiles.reshape(*held, *shard.shape)
    turned = sorted(range(len(turns)), key=lambda place: turns[len(turns) - 1 - place])
    return tiles.transpose(*turned, *range(len(turns), tiles.ndim)).reshape(-1, *shard.shape)


def gathered_by_axis(shard, axes, turns, dim):
    return in_order(all_blocks(shard, axes, turns), dim)


def send_out(message):
    return lax.all_to_all(message, GRP_WAVE, split_axis=1, concat_axis=1, tiled=True)


def send_home(message):
    return lax.all_to_all(message, GRP_WAVE, split_axis=1, concat_axis=1, tiled=True)


def solve_columns(inverses, right_side, low_mask, split):
    upper = jnp.einsum(
        "jkl,lajc->kajc", inverses[:, 1], right_side, preferred_element_type=jnp.float32
    )
    lower = jnp.einsum(
        "jkl,lajc->kajc",
        inverses[:, 0],
        right_side[..., :split],
        preferred_element_type=jnp.float32,
    )
    first = jnp.where(low_mask[None, :, :, :split], lower, upper[..., :split])
    return jnp.concatenate([first, upper[..., split:]], axis=-1).astype(jnp.bfloat16)


def shards(
    state,
    held_orders,
    pair_lows,
    inverses,
    height_operator,
    pressure_column,
    thermal_response_matrix,
    mass_row,
):
    layer_heights_count = height_operator.shape[0]
    pair_count = pair_lows.shape[0]
    slot_count = held_orders.shape[0]
    devices = lax.axis_size("grp") * lax.axis_size(WAVE)
    truncation = 2 * pair_count * devices - 1
    slot_width = 2 * (truncation + 2)
    denom = float(truncation * (truncation + 1))
    fill_col = slot_count * slot_width
    all_lows = gathered_by_axis(pair_lows, (("grp", "wave_0", "wave_1"), "wave_2"), (0, 1), 0)
    own_low = pair_lows.reshape(1, pair_count, 1)
    all_orders = gathered_by_axis(held_orders, GRP_WAVE, (0, 1, 2, 3), 0)
    low_grid = all_lows.reshape(devices, pair_count, 1, 1)
    orders = held_orders.reshape(1, 1, slot_count, 1)
    halves = jnp.arange(2, dtype=jnp.int32).reshape(1, 1, 1, 2)
    slot_ids = jnp.arange(slot_count, dtype=jnp.int32).reshape(1, 1, slot_count, 1)
    live = orders >= 0

    def place(position):
        spot = slot_ids * slot_width + 2 * position + halves
        return jnp.where(live, spot, fill_col).reshape(devices, pair_count, -1)

    first = place(jnp.where(orders <= low_grid, low_grid - orders, truncation + 1 - low_grid))
    second = place(truncation - low_grid - orders)
    hit = orders == low_grid
    found = jnp.any(hit, axis=2)
    slot_hit = jnp.sum(jnp.where(hit, slot_ids, 0), axis=2)
    extra = slot_hit * slot_width + 2 * (truncation + 1 - low_grid[:, :, 0]) + halves[:, :, 0]
    extra = jnp.where(found, extra, fill_col)
    column = jnp.concatenate([first, second, extra], axis=2).reshape(-1)
    source_orders = all_orders.reshape(devices, 1, slot_count, 1)
    low_first = jnp.broadcast_to(
        source_orders <= own_low[..., None], (devices, pair_count, slot_count, 2)
    ).reshape(devices, pair_count, -1)
    low_mask = jnp.concatenate(
        [low_first, jnp.zeros((devices, pair_count, 2 * slot_count + 2), jnp.bool_)], axis=2
    )
    split = 2 * slot_count
    per_pair = low_mask.shape[2]
    recv_shape = (devices, pair_count, per_pair)
    divergence = state[:layer_heights_count]
    thermal_state_array = state[layer_heights_count : 2 * layer_heights_count]
    pressure = state[2 * layer_heights_count]
    coeff_index = (jnp.arange(slot_width, dtype=jnp.int32) // 2)[None, :]
    order_col = held_orders[:, None]
    degree = jnp.where(
        coeff_index <= truncation - order_col, order_col + coeff_index, coeff_index - 1
    )
    lap_scale = ((degree * (degree + 1)).astype(jnp.float32) / denom).reshape(-1)
    height_drive_term = jnp.dot(
        height_operator, thermal_state_array, preferred_element_type=jnp.float32
    )
    height_drive_term = (
        height_drive_term
        + pressure_column.astype(jnp.float32)[:, None] * pressure.astype(jnp.float32)[None, :]
    )
    right_side = (divergence.astype(jnp.float32) + lap_scale[None, :] * height_drive_term).astype(
        jnp.bfloat16
    )
    message = jnp.take(right_side, column, axis=1, mode="fill", fill_value=0)
    arriving_arrays = send_out(message).reshape((layer_heights_count,) + recv_shape)
    div_sent = solve_columns(inverses, arriving_arrays, low_mask, split).reshape(
        layer_heights_count, -1
    )
    returned = send_home(div_sent)
    next_spreading_rate = (
        jnp.zeros((layer_heights_count, fill_col), jnp.bfloat16)
        .at[:, column]
        .set(returned, mode="drop")
    )
    next_thermal_state = (
        thermal_state_array.astype(jnp.float32)
        - jnp.dot(thermal_response_matrix, next_spreading_rate, preferred_element_type=jnp.float32)
    ).astype(jnp.bfloat16)
    surface_mass_next = (
        pressure.astype(jnp.float32)
        - jnp.dot(mass_row, next_spreading_rate, preferred_element_type=jnp.float32)
    ).astype(jnp.bfloat16)
    live_slot = jnp.repeat(held_orders >= 0, slot_width)[None, :]
    result = jnp.concatenate(
        [next_spreading_rate, next_thermal_state, surface_mass_next[None, :]], axis=0
    )
    return jnp.where(live_slot, result, jnp.zeros_like(result))


def solution(mesh):
    torus = Mesh(
        mesh.devices.reshape(mesh.shape["grp"], 4, 4, 2), ("grp", "wave_0", "wave_1", "wave_2")
    )
    placed = (
        P(None, GRP_WAVE),
        P(GRP_WAVE),
        P(GRP_WAVE),
        P(GRP_WAVE, None, None, None),
        P(),
        P(),
        P(),
        P(),
    )
    return jax.shard_map(
        shards, mesh=torus, in_specs=placed, out_specs=P(None, GRP_WAVE), check_vma=False
    )
```

profile of v0, /device:TPU:1, one launch (start us, length us, event | category | flops | bytes accessed | tf_op | source)
XLA Modules:
  0.0 343.0 jit_solution(1832600771421519429)
XLA Ops:
  0.0 1.3 dynamic-slice
  1.9 0.9 dynamic-update-slice
  2.8 20.8 %all-reduce = s32[192]{0:T(256)S(1)} all-reduce(s32[192]{0:T(256)S(1)} %dynamic-update-slice), channel_id=2, replica_groups=mesh['grp'=4,'wave_0'=4,'wave_1'=4,'wave_2'=2] {'grp','wave_0','wave_1'}, use_global_device_ids=true, to_apply=%add | all-reduce | flops 192 | bytes 1536
  23.8 7.4 %all-gather.2 = s32[2,64,3]{1,2,0:T(4,128)S(1)} all-gather(s32[1,64,3]{1,2,0:T(4,128)S(1)} %copy.56), channel_id=1, replica_groups=mesh['grp'=4,'wave_0'=4,'wave_1'=4,'wave_2'=2] {'wave_2'}, dimensions={0}, use_global_device_ids=true | all-gather | bytes 2304 | tf_op jit(solution)/shard_map/all_gather | solution.py:20
  31.4 0.7 broadcast_compare_fusion.1
  32.1 0.7 fusion.15
  32.8 0.7 compare_reduce_fusion
  33.6 0.7 broadcast_subtract_fusion.2
  34.3 0.7 multiply_add_fusion.1
  35.6 0.2 reshape.227
  36.0 0.7 add_select_fusion
  36.8 1.0 convert_reduce_fusion
  37.8 0.7 convert_element_type.37
  38.5 3.9 %fusion.4 = bf16[137,7690]{1,0:T(8,128)(2,1)S(1)} fusion(bf16[137,137]{1,0:T(8,128)(2,1)S(1)} %copy-done, f32[7690]{0:T(1024)S(1)} %convert_reduce_fusion, f32[137]{0:T(256)S(1)} %convert_element_type.37, f32[7690]{0:T(1024)S(1)} %fusion.11, bf16[275,7690]{1,0:T(8,128)(2,1)} %param.8), kind=kOutput, calls=%fused_computation.8 | convolution fusion | flops 294988448 | bytes 6704074 | tf_op jit(solution)/shard_map/dot_general | solution.py:111
  42.4 3.7 %copy.67 = bf16[137,7690]{0,1:T(8,128)(2,1)} copy(bf16[137,7690]{1,0:T(8,128)(2,1)S(1)} %fusion.4) | data formatting | bytes 4214120 | tf_op jit(solution)/shard_map/convert_element_type | solution.py:118
  46.1 22.6 %gather_fusion = bf16[8448,137]{1,0:T(8,128)(2,1)} fusion(bf16[137,7690]{0,1:T(8,128)(2,1)} %copy.67, s32[9216]{0:T(1024)S(1)} %pad_clamp_fusion), kind=kCustom, calls=%fused_computation | custom fusion | bytes 4663296 | tf_op jit(solution)/shard_map/jit(_take)/gather | solution.py:121
  68.8 4.6 %copy.68 = bf16[137,8448]{1,0:T(8,128)(2,1)S(1)} copy(bf16[137,8448]{0,1:T(8,128)(2,1)} %bitcast.62) | data formatting | bytes 4629504 | tf_op jit(solution)/shard_map/jit(_take)/gather | solution.py:121
  73.4 16.8 %gather.7 = bf16[137,128,66]{2,1,0:T(8,128)(2,1)} reshape(bf16[137,8448]{1,0:T(8,128)(2,1)S(1)} %copy.68) | data formatting | bytes 4629504 | tf_op jit(solution)/shard_map/jit(_take)/gather | solution.py:121
  90.3 2.6 broadcast_select_fusion
  92.9 5.0 %copy.88 = bf16[137,128,66]{2,0,1:T(8,128)(2,1)} copy(bf16[137,128,66]{2,1,0:T(8,128)(2,1)S(1)} %broadcast_select_fusion) | data formatting | bytes 4629504 | tf_op jit(solution)/shard_map/jit(_take)/select_n | solution.py:121
  97.9 17.0 %reshape.283 = bf16[128,2,4521]{2,1,0:T(2,128)(2,1)} reshape(bf16[128,137,66]{2,1,0:T(8,128)(2,1)} %bitcast.58) | data formatting | bytes 4629504
  115.0 3.9 %all-to-all-start = ((bf16[128,2,4521]{2,1,0:T(2,128)(2,1)}), bf16[128,2,4521]{2,1,0:T(2,128)(2,1)S(1)}, u32[]{:S(2)}, u32[]{:S(2)}) async-start(bf16[128,2,4521]{2,1,0:T(2,128)(2,1)} %reshape.283), calls=%async_computation | async-start | bytes 4718592 | tf_op jit(solution)/shard_map/all_to_all | solution.py:32
  118.9 0.7 dynamic-slice.1
  120.3 0.2 dynamic-update-slice.1
  120.6 13.8 %all-reduce.1 = s32[20]{0:T(128)S(1)} all-reduce(s32[20]{0:T(128)S(1)} %dynamic-update-slice.1), channel_id=3, replica_groups=mesh['grp'=4,'wave_0'=4,'wave_1'=4,'wave_2'=2] {'grp'}, use_global_device_ids=true, to_apply=%add.1 | all-reduce | flops 20 | bytes 160
  134.5 15.7 %all-gather.3 = s32[4,4,5]{2,1,0:T(4,128)S(1)} all-gather(s32[1,4,5]{2,1,0:T(4,128)S(1)} %reshape.258), channel_id=1, replica_groups=mesh['grp'=4,'wave_0'=4,'wave_1'=4,'wave_2'=2] {'wave_0'}, dimensions={0}, use_global_device_ids=true | all-gather | bytes 400 | tf_op jit(solution)/shard_map/all_gather | solution.py:20
  150.2 16.4 %all-gather.4 = s32[4,16,5]{1,2,0:T(8,128)S(1)} all-gather(s32[1,16,5]{1,2,0:T(8,128)S(1)} %copy.79), channel_id=1, replica_groups=mesh['grp'=4,'wave_0'=4,'wave_1'=4,'wave_2'=2] {'wave_1'}, dimensions={0}, use_global_device_ids=true | all-gather | bytes 1600 | tf_op jit(solution)/shard_map/all_gather | solution.py:20
  166.7 10.1 %all-gather.5 = s32[2,64,5]{1,2,0:T(8,128)S(1)} all-gather(s32[1,64,5]{1,2,0:T(8,128)S(1)} %reshape.262), channel_id=1, replica_groups=mesh['grp'=4,'wave_0'=4,'wave_1'=4,'wave_2'=2] {'wave_2'}, dimensions={0}, use_global_device_ids=true | all-gather | bytes 3840 | tf_op jit(solution)/shard_map/all_gather | solution.py:20
  177.0 0.3 copy.63
  177.6 1.3 fusion.16
  178.9 10.2 %reshape.284 = bf16[128,137,66]{2,1,0:T(8,128)(2,1)} reshape(bf16[128,2,4521]{2,1,0:T(2,128)(2,1)S(1)} %all-to-all-done) | data formatting | bytes 4629504
  189.1 6.0 %copy.70 = bf16[137,128,66]{1,0,2:T(8,128)(2,1)S(1)} copy(bf16[137,128,66]{2,0,1:T(8,128)(2,1)} %bitcast.59) | data formatting | bytes 4629504 | tf_op jit(solution)/shard_map/all_to_all | solution.py:32
  195.1 0.8 convolution_bitcast_fusion.1
  196.1 0.4 fusion.5
  196.6 0.2 pad_maximum_fusion
  196.8 4.9 %copy.73 = bf16[137,128,66]{2,0,1:T(8,128)(2,1)} copy(bf16[137,128,66]{1,0,2:T(8,128)(2,1)S(1)} %bitcast.66) | data formatting | bytes 4629504 | tf_op jit(solution)/shard_map/convert_element_type | solution.py:50
  201.8 16.8 %reshape.285 = bf16[128,2,4521]{2,1,0:T(2,128)(2,1)} reshape(bf16[128,137,66]{2,1,0:T(8,128)(2,1)} %bitcast.60) | data formatting | bytes 4629504
  218.6 5.8 %all-to-all-start.1 = ((bf16[128,2,4521]{2,1,0:T(2,128)(2,1)}), bf16[128,2,4521]{2,1,0:T(2,128)(2,1)S(1)}, u32[]{:S(2)}, u32[]{:S(2)}) async-start(bf16[128,2,4521]{2,1,0:T(2,128)(2,1)} %reshape.285), calls=%async_computation.1 | async-start | bytes 4718592 | tf_op jit(solution)/shard_map/all_to_all | solution.py:36
  224.7 32.9 %all-to-all-done.1 = bf16[128,2,4521]{2,1,0:T(2,128)(2,1)S(1)} async-done(((bf16[128,2,4521]{2,1,0:T(2,128)(2,1)}), bf16[128,2,4521]{2,1,0:T(2,128)(2,1)S(1)}, u32[]{:S(2)}, u32[]{:S(2)}) %all-to-all-start.1) | async-done | bytes 2314784 | tf_op jit(solution)/shard_map/all_to_all | solution.py:36
  257.6 10.2 %reshape.286 = bf16[128,137,66]{2,1,0:T(8,128)(2,1)} reshape(bf16[128,2,4521]{2,1,0:T(2,128)(2,1)S(1)} %all-to-all-done.1) | data formatting | bytes 4629504
  267.8 5.6 %copy.74 = bf16[137,128,66]{2,1,0:T(8,128)(2,1)} copy(bf16[137,128,66]{2,0,1:T(8,128)(2,1)} %bitcast.61) | data formatting | bytes 4629504 | tf_op jit(solution)/shard_map/all_to_all | solution.py:36
  273.4 7.4 %reshape.241 = bf16[137,8448]{1,0:T(8,128)(2,1)S(1)} reshape(bf16[137,128,66]{2,1,0:T(8,128)(2,1)} %copy.74) | data formatting | bytes 4629504 | tf_op jit(solution)/shard_map/all_to_all | solution.py:36
  280.8 3.8 %copy.75 = bf16[8448,137]{1,0:T(8,128)(2,1)} copy(bf16[8448,137]{0,1:T(8,128)(2,1)S(1)} %bitcast.65) | data formatting | bytes 4629504 | tf_op jit(solution)/shard_map/all_to_all | solution.py:36
  284.6 44.6 %scatter_custom_fusion = bf16[137,7690]{0,1:T(8,128)(2,1)} fusion(s32[8448]{0:T(1024)S(1)} %fusion.9, bf16[8448,137]{1,0:T(8,128)(2,1)} %copy.75, bf16[]{:T(256)} %constant.21.clone.1), kind=kCustom, calls=%fused_computation.17 | custom fusion | bytes 2107572 | tf_op jit(solution)/shard_map/scatter | solution.py:130
  329.2 4.5 %copy.76 = bf16[137,7690]{1,0:T(8,128)(2,1)S(1)} copy(bf16[137,7690]{0,1:T(8,128)(2,1)} %scatter_custom_fusion) | data formatting | bytes 4214120 | tf_op jit(solution)/shard_map/scatter | solution.py:130
  333.8 4.5 %fusion.3 = bf16[137,7690]{1,0:T(8,128)(2,1)S(1)} fusion(bf16[137,7690]{0,1:T(8,128)(2,1)} %scatter_custom_fusion, bf16[137,137]{1,0:T(8,128)(2,1)S(1)} %copy-done.7, bf16[275,7690]{1,0:T(8,128)(2,1)} %param.8), kind=kOutput, calls=%fused_computation.7 | convolution fusion | flops 291827840 | bytes 6358718 | tf_op jit(solution)/shard_map/dot_general | solution.py:134
  338.3 1.1 convolution_reduce_fusion
  339.5 3.3 maximum_select_fusion
  (65 shorter events, 2.4 us)
Async XLA Ops:
  0.0 38.5 %copy-start = (bf16[137,137]{1,0:T(8,128)(2,1)S(1)}, bf16[137,137]{1,0:T(8,128)(2,1)}, u32[]{:S(2)}) copy-start(bf16[137,137]{1,0:T(8,128)(2,1)} %param.12) | copy-start | bytes 112618
  115.0 4.0 %copy-start.9 = (u32[128]{0:T(128)S(1)}, u32[128]{0:T(128)}, u32[]{:S(2)}) copy-start(u32[128]{0:T(128)} %constant.72) | copy-start | bytes 1540
  115.0 5.3 %copy-start.5 = (s32[5]{0:T(128)S(1)}, s32[5]{0:T(128)}, u32[]{:S(2)}) copy-start(s32[5]{0:T(128)} %param.9) | copy-start | bytes 64
  115.0 62.4 %copy-start.6 = (s32[3]{0:T(128)S(1)}, s32[3]{0:T(128)}, u32[]{:S(2)}) copy-start(s32[3]{0:T(128)} %param.10) | copy-start | bytes 40
  115.0 62.6 %copy-start.3 = (bf16[3,2,137,137]{3,1,2,0:T(2,128)(2,1)S(1)}, bf16[3,2,137,137]{3,1,2,0:T(2,128)(2,1)}, u32[]{:S(2)}) copy-start(bf16[3,2,137,137]{3,1,2,0:T(2,128)(2,1)} %param.11) | copy-start | bytes 675688
  115.0 63.9 %all-to-all-start = ((bf16[128,2,4521]{2,1,0:T(2,128)(2,1)}), bf16[128,2,4521]{2,1,0:T(2,128)(2,1)S(1)}, u32[]{:S(2)}, u32[]{:S(2)}) async-start(bf16[128,2,4521]{2,1,0:T(2,128)(2,1)} %reshape.283), calls=%async_computation | async-start | bytes 4718592 | tf_op jit(solution)/shard_map/all_to_all | solution.py:32
  195.1 1.0 copy-start.4
  218.6 5.9 %copy-start.8 = (bf16[137]{0:T(256)(128)(2,1)S(1)}, bf16[137]{0:T(256)(128)(2,1)}, u32[]{:S(2)}) copy-start(bf16[137]{0:T(256)(128)(2,1)} %param.15) | copy-start | bytes 826
  218.6 39.0 %all-to-all-start.1 = ((bf16[128,2,4521]{2,1,0:T(2,128)(2,1)}), bf16[128,2,4521]{2,1,0:T(2,128)(2,1)S(1)}, u32[]{:S(2)}, u32[]{:S(2)}) async-start(bf16[128,2,4521]{2,1,0:T(2,128)(2,1)} %reshape.285), calls=%async_computation.1 | async-start | bytes 4718592 | tf_op jit(solution)/shard_map/all_to_all | solution.py:36
  329.2 4.5 %copy-start.7 = (bf16[137,137]{1,0:T(8,128)(2,1)S(1)}, bf16[137,137]{1,0:T(8,128)(2,1)}, u32[]{:S(2)}) copy-start(bf16[137,137]{1,0:T(8,128)(2,1)} %param.14) | copy-start | bytes 112618
  333.8 4.5 %copy-start.2 = (bf16[137,7690]{0,1:T(8,128)(2,1)S(1)}, bf16[137,7690]{0,1:T(8,128)(2,1)}, u32[]{:S(2)}) copy-start(bf16[137,7690]{0,1:T(8,128)(2,1)} %scatter_custom_fusion) | copy-start | bytes 6321184
  339.5 3.4 copy-start.1
where the time goes:
time: 348 us; the launch traced here: 343 us
  local copies, waits for them, and re-layouts  191 us (55%)
  blocking collectives  84.2 us (24%)
  waiting for transfers between devices  32.9 us (9%)
  other arithmetic  12.4 us (4%)
  matrix products  10.8 us (3%)
  starting transfers between devices  9.79 us (3%)
    unnamed x36, local copies, waits for them, and re-layouts  57.9 us
    all_gather x4, blocking collectives, all_blocks(): tiles = lax.all_gather(tiles, axes[k], axis=0, tiled=True)  49.6 us
    scatter x2, local copies, waits for them, and re-layouts, shards(): next_spreading_rate = jnp.zeros((layer_heights_count, fill_col), jnp.bflo...  49.1 us
    gather x3, local copies, waits for them, and re-layouts, shards(): message = jnp.take(right_side, column, axis=1, mode='fill', fill_value=0)  44 us
    unnamed x2, blocking collectives  34.6 us
    all_to_all x1, waiting for transfers between devices, send_home(): lax.all_to_all(message, GRP_WAVE, split_axis=1, concat_axis=1, tiled=True)  32.9 us
    all_to_all x3, local copies, waits for them, and re-layouts, send_home(): lax.all_to_all(message, GRP_WAVE, split_axis=1, concat_axis=1, tiled=True)  16.8 us
  transfers between devices with their start and end apart: 2, of which 1 were waited for; matrix products, arithmetic and copies ran while one was open for 1% of the time, Pallas kernels for 0%

commit v1 on v0

v1 whole, which is shorter than its diff:
```python
import functools

import jax
import jax.numpy as jnp
from jax import lax
from jax.experimental import pallas as pl
from jax.experimental.pallas import tpu as pltpu
from jax.sharding import Mesh
from jax.sharding import PartitionSpec as P

AXES = ("grp", "wave_0", "wave_1", "wave_2")
MESH = pl.DeviceIdType.MESH
BF16 = jnp.bfloat16
F32 = jnp.float32
LEV = 137
REM = LEV - 128
HALF = 384
TRUNC = 767
SLOTS = 5
WIDTH = 2 * (TRUNC + 2)
COLS = SLOTS * WIDTH
ROWS = 7696
PAIR_ROWS = 24
CHUNK = 8 * PAIR_ROWS
MSG = 224
UNIT = 320
LANES14 = 14
TILE = 1024
TILES = 8


def list_id(j, t, e):
    return j * 4 + t * 2 + e


def partner(core, p):
    even = p % 2
    return (1 - core) * (p + 1 - 2 * even) + core * (3 - p)


def solver_coords(pos, core, j, t, e):
    dest_core = (core + e) % 2
    pa = pos[j] if t == 0 else partner(dest_core, pos[j])
    return [pa if d == j else pos[d] for d in range(3)], dest_core


def source_coords(pos, core, j, rc, rb, ra):
    a, b, c = j, (j + 1) % 3, (j + 2) % 3
    out = [None, None, None]
    pa = pos[a]
    out[a] = pa + ra * (partner(1 - core, pa) - pa)
    out[b] = (pos[b] + 4 - rb) % 4
    out[c] = (pos[c] + 4 - rc) % 4
    return out


def slot_rows(low, order):
    first = jnp.where(order <= low, 2 * (low - order), 2 * (TRUNC + 1 - low))
    second = 2 * (TRUNC - low - order)
    return first, second


def pair_rows(low, orders, miss):
    rows = []
    extra = miss
    for s in range(SLOTS):
        first, second = slot_rows(low, orders[s])
        rows.append((2 * s, s * WIDTH + first))
        rows.append((2 * SLOTS + 2 * s, s * WIDTH + second))
        extra = jnp.where(orders[s] == low, s * WIDTH + 2 * (TRUNC + 1 - low), extra)
    rows.append((4 * SLOTS, extra))
    return rows


def exchange_kernel(
    units_hbm, meta_hbm, xm_hbm, xr_hbm, held,
    yr_out, meta_out,
    G, META, METAS, XM, XR, SND, RCV, YS, YR, TM, TR, MV, RA,
    in_sem, g_send, g_recv, m_send, m_recv, f_send, f_recv, b_send, b_recv, out_sem,
):
    pos = [lax.axis_index(AXES[d]) for d in range(3)]
    core = lax.axis_index(AXES[3])

    def device(coords, c):
        return {AXES[0]: coords[0], AXES[1]: coords[1], AXES[2]: coords[2], AXES[3]: c}

    def shifted(d, delta):
        return [(pos[k] + 4 + delta) % 4 if k == d else pos[k] for k in range(3)]

    own_meta = META.at[core, pos[2], pos[1], pos[0]]
    loads = [
        pltpu.make_async_copy(units_hbm, G.at[:, 0, 0, 0], in_sem.at[0]),
        pltpu.make_async_copy(meta_hbm, own_meta, in_sem.at[1]),
        pltpu.make_async_copy(xm_hbm, XM, in_sem.at[2]),
        pltpu.make_async_copy(xr_hbm, XR, in_sem.at[3]),
    ]
    for load in loads:
        load.start()

    barrier = pltpu.get_barrier_semaphore()
    peers = []
    for d in range(3):
        for delta in (1, -1):
            peers.append((shifted(d, delta), core))
            peers.append((shifted(d, delta), 1 - core))
        peers.append((shifted(d, 2), core))
    peers.append((pos, 1 - core))
    for coords, c in peers:
        pl.semaphore_signal(barrier, inc=1, device_id=device(coords, c), device_id_type=MESH)
    pl.semaphore_wait(barrier, len(peers))

    def unit_copy(j, dest):
        rc, rb, ra = dest
        a, b, c = j, (j + 1) % 3, (j + 2) % 3
        if dest == (0, 0, 1):
            src = (0, 0, 0)
            coords = [partner(1 - core, pos[k]) if k == a else pos[k] for k in range(3)]
        elif rc == 0:
            ring, step, k = b, rb, 1
        else:
            ring, step, k = c, rc, 0
        if dest != (0, 0, 1):
            forward = {1: (0, 1), 3: (0, -1), 2: (1, 1) if ra == 0 else (3, -1)}[step]
            src = list(dest)
            src[k] = forward[0]
            src = tuple(src)
            coords = shifted(ring, forward[1])
        return src, pltpu.make_async_remote_copy(
            src_ref=G.at[(j,) + src],
            dst_ref=G.at[(j,) + dest],
            send_sem=g_send.at[(j,) + dest],
            recv_sem=g_recv.at[(j,) + dest],
            device_id=device(coords, core),
            device_id_type=MESH,
        )

    here = {(j, 0, 0, 0) for j in range(3)}
    sent = []

    def need(j, unit):
        if (j,) + unit not in here:
            here.add((j,) + unit)
            unit_copy(j, unit)[1].wait_recv()

    def send(*dests):
        for dest in dests:
            for j in range(3):
                src, copy = unit_copy(j, dest)
                need(j, src)
                copy.start()
                sent.append(copy)

    def meta_copies(stage):
        out = []
        if stage < 3:
            d = stage
            index = (core, pos[2], pos[1], pos[0])[: 4 - d]
            for delta in (1, 2, 3):
                out.append((index, device(shifted(d, delta), core), 3 * d + delta - 1))
        else:
            out.append(((core,), device(pos, 1 - core), 9))
        return out

    def meta_copy(index, dev, sem):
        ref = META.at[index]
        return pltpu.make_async_remote_copy(
            src_ref=ref, dst_ref=ref, send_sem=m_send.at[sem], recv_sem=m_recv.at[sem],
            device_id=dev, device_id_type=MESH,
        )

    def meta_start(stage):
        for item in meta_copies(stage):
            copy = meta_copy(*item)
            copy.start()
            sent.append(copy)

    def meta_wait(stage):
        for item in meta_copies(stage):
            meta_copy(*item).wait_recv()

    loads[1].wait()
    meta_start(0)
    loads[0].wait()
    send((0, 0, 1), (0, 1, 0), (0, 3, 0), (1, 0, 0), (3, 0, 0))
    TM[...] = jnp.zeros_like(TM)
    TR[...] = jnp.zeros_like(TR)
    meta_wait(0)
    meta_start(1)
    meta_wait(1)
    meta_start(2)
    meta_wait(2)
    meta_start(3)
    send((0, 1, 1), (0, 3, 1), (1, 0, 1), (3, 0, 1))
    meta_wait(3)
    table = pltpu.make_async_copy(META, METAS, in_sem.at[4])
    table.start()
    meta_store = pltpu.make_async_copy(META, meta_out, in_sem.at[5])
    meta_store.start()
    table.wait()
    loads[2].wait()
    loads[3].wait()

    orders = [held[s] for s in range(SLOTS)]

    def low_of(coords, c, j):
        return METAS[c, coords[2], coords[1], coords[0], 0, j]

    def pack(j, t, e):
        dest, dest_core = solver_coords(pos, core, j, t, e)
        l = list_id(j, t, e)
        target = RCV if t + e == 0 else SND

        def body(rc, carry):
            for u in range(8):
                src = source_coords(dest, dest_core, j, rc, u // 2, u % 2)
                low = low_of(src, dest_core, j)
                for at, row in pair_rows(low, orders, 0):
                    put = PAIR_ROWS * u + at
                    TM[put : put + 2, :] = XM[pl.ds(row, 2), :]
                    TR[put : put + 2, :] = XR[pl.ds(row, 2), :]
            target[l, rc, 0:CHUNK, :] = TM[...].astype(BF16)
            tail = TR[0:PAIR_ROWS, :]
            for u in range(1, 8):
                tail += pltpu.roll(TR[PAIR_ROWS * u : PAIR_ROWS * (u + 1), :], 16 * u, 1)
            tail = jnp.concatenate([tail, jnp.zeros((MSG - CHUNK - PAIR_ROWS, 128), F32)], axis=0)
            target[l, rc, CHUNK:MSG, :] = tail.astype(BF16)
            return carry

        lax.fori_loop(0, 4, body, 0)
        if t + e:
            copy = forward_copy(j, t, e)
            copy.start()
            sent.append(copy)

    def forward_copy(j, t, e):
        dest, dest_core = solver_coords(pos, core, j, t, e)
        l = list_id(j, t, e)
        return pltpu.make_async_remote_copy(
            src_ref=SND.at[l], dst_ref=RCV.at[l], send_sem=f_send.at[l], recv_sem=f_recv.at[l],
            device_id=device(dest, dest_core), device_id_type=MESH,
        )

    def origin(j, t, e):
        pa = pos[j] if t == 0 else partner(core, pos[j])
        return [pa if d == j else pos[d] for d in range(3)], (core + e) % 2

    def return_copy(j, t, e, rc):
        l = list_id(j, t, e)
        coords, c = origin(j, t, e)
        return pltpu.make_async_remote_copy(
            src_ref=YS.at[l, rc], dst_ref=YR.at[l, rc], send_sem=b_send.at[l, rc], recv_sem=b_recv.at[l, rc],
            device_id=device(coords, c), device_id_type=MESH,
        )

    every = [(t, e) for t in (1, 0) for e in (0, 1)]
    row_id = lax.broadcasted_iota(jnp.int32, (PAIR_ROWS, 128), 0)

    def order_rows(j):
        for t, e in every:
            coords, c = origin(j, t, e)
            rows = jnp.full((PAIR_ROWS, 128), HALF + 1, jnp.int32)
            for s in range(SLOTS):
                order = METAS[c, coords[2], coords[1], coords[0], 0, 8 + s]
                rows = jnp.where(row_id // 2 == s, order, rows)
            MV[j, PAIR_ROWS * (2 * t + e) : PAIR_ROWS * (2 * t + e + 1), :] = rows

    lane = lax.broadcasted_iota(jnp.int32, (4 * PAIR_ROWS, 128), 1)

    def solve(j, rc):
        RA[...] = jnp.zeros_like(RA)

        def body(rb, carry):
            rows = pl.ds(pl.multiple_of(2 * PAIR_ROWS * rb, 16), 2 * PAIR_ROWS)
            mains = [RCV[list_id(j, k // 2, k % 2), rc, rows, :].astype(F32) for k in range(4)]
            tails = jnp.concatenate(
                [RCV[list_id(j, k // 2, k % 2), rc, CHUNK:MSG, :].astype(F32)[:PAIR_ROWS] for k in range(4)], axis=0
            )
            solved = []
            for ra in range(2):
                u = 2 * rb + ra
                low = low_of(source_coords(pos, core, j, rc, rb, ra), core, j)
                unit = G.at[j, rc, rb, ra]
                x = jnp.concatenate([m[PAIR_ROWS * ra : PAIR_ROWS * (ra + 1)] for m in mains], axis=0)
                is_low = MV[j] <= low
                main = jnp.concatenate([jnp.where(is_low, x, 0.0), jnp.where(is_low, 0.0, x)], axis=1).astype(BF16)
                tail_low = pltpu.roll(tails, (128 - 16 * u) % 128, 1)
                tail_high = pltpu.roll(tails, (144 - 16 * u) % 128, 1)
                tail = jnp.where(
                    lane < 16,
                    jnp.where(is_low, tail_low, 0.0),
                    jnp.where(lane < 32, jnp.where(is_low, 0.0, tail_high), 0.0),
                ).astype(BF16)
                strips = [unit[288:304, :].astype(F32), unit[304:320, :].astype(F32)]
                strip = jnp.concatenate(
                    [
                        pltpu.roll(strips[g // LANES14], (128 - REM * (g % LANES14)) % 128, 1)
                        for g in range(18)
                    ],
                    axis=0,
                ).astype(BF16)
                weights = jnp.concatenate([unit[0:256, :], strip[0:256]], axis=1)
                low_weights = jnp.concatenate([unit[256:288, :], strip[256:288]], axis=1)
                y = jnp.dot(main, weights, preferred_element_type=F32) + jnp.dot(
                    tail[:, 0:32], low_weights, preferred_element_type=F32
                )
                solved.append(y[:, 0:128])
                shifted_tail = pltpu.roll(y[:, 128:256], 16 * u, 1)
                keep = (lane >= 16 * u) & (lane < 16 * u + REM)
                RA[...] += jnp.where(keep, shifted_tail, 0.0)
            for k in range(4):
                l = list_id(j, k // 2, k % 2)
                part = slice(PAIR_ROWS * k, PAIR_ROWS * (k + 1))
                (YR if k == 0 else YS)[l, rc, rows, :] = jnp.concatenate(
                    [solved[0][part], solved[1][part]], axis=0
                ).astype(BF16)
            return carry

        lax.fori_loop(0, 4, body, 0)
        for k in range(4):
            l = list_id(j, k // 2, k % 2)
            part = jnp.concatenate(
                [RA[PAIR_ROWS * k : PAIR_ROWS * (k + 1), :], jnp.zeros((MSG - CHUNK - PAIR_ROWS, 128), F32)], axis=0
            )
            (YR if k == 0 else YS)[l, rc, CHUNK:MSG, :] = part.astype(BF16)
            if k:
                copy = return_copy(j, k // 2, k % 2, rc)
                copy.start()
                sent.append(copy)

    for j in range(3):
        pack(j, 1, 0)
        pack(j, 1, 1)
        if j == 0:
            send((0, 2, 0), (1, 1, 0), (3, 1, 0), (1, 3, 0), (3, 3, 0))
        elif j == 1:
            send((0, 2, 1), (1, 1, 1), (3, 1, 1), (1, 3, 1), (3, 3, 1))
        else:
            send((2, 0, 0), (2, 0, 1))
    for j in range(3):
        pack(j, 0, 1)
    send((1, 2, 0), (3, 2, 0), (1, 2, 1), (3, 2, 1))
    for j in range(3):
        pack(j, 0, 0)
        order_rows(j)
    send((2, 1, 0), (2, 1, 1), (2, 3, 0), (2, 3, 1))

    got = set()

    def solve_ready(j, rc):
        for t, e in every:
            if t + e and (j, t, e) not in got:
                got.add((j, t, e))
                forward_copy(j, t, e).wait_recv()
        for rb in range(4):
            for ra in range(2):
                need(j, (rc, rb, ra))
        solve(j, rc)

    for j in range(3):
        solve_ready(j, 0)
    send((2, 2, 0), (2, 2, 1))
    for rc in (1, 3, 2):
        for j in range(3):
            solve_ready(j, rc)
    for j in range(3):
        for rc in range(4):
            for t, e in every:
                if t + e:
                    return_copy(j, t, e, rc).wait_recv()
    done = pltpu.make_async_copy(YR, yr_out, out_sem)
    done.start()
    done.wait()
    meta_store.wait()
    for copy in sent:
        copy.wait_send()


def exchange(units, meta, xm, xr, held):
    any_space = pl.BlockSpec(memory_space=pl.ANY)
    messages = pltpu.VMEM((12, 4, MSG, 128), BF16)
    return pl.pallas_call(
        exchange_kernel,
        out_shape=(
            jax.ShapeDtypeStruct((12, 4, MSG, 128), BF16),
            jax.ShapeDtypeStruct((2, 4, 4, 4, 1, 128), jnp.int32),
        ),
        in_specs=[any_space] * 4 + [pl.BlockSpec(memory_space=pltpu.SMEM)],
        out_specs=(any_space, any_space),
        scratch_shapes=[
            pltpu.VMEM((3, 4, 4, 2, UNIT, 128), BF16),
            pltpu.VMEM((2, 4, 4, 4, 1, 128), jnp.int32),
            pltpu.SMEM((2, 4, 4, 4, 1, 128), jnp.int32),
            pltpu.VMEM((ROWS, 128), F32),
            pltpu.VMEM((ROWS, 128), F32),
            messages,
            messages,
            messages,
            messages,
            pltpu.VMEM((CHUNK, 128), F32),
            pltpu.VMEM((CHUNK, 128), F32),
            pltpu.VMEM((3, 4 * PAIR_ROWS, 128), jnp.int32),
            pltpu.VMEM((4 * PAIR_ROWS, 128), F32),
            pltpu.SemaphoreType.DMA((6,)),
            pltpu.SemaphoreType.DMA((3, 4, 4, 2)),
            pltpu.SemaphoreType.DMA((3, 4, 4, 2)),
            pltpu.SemaphoreType.DMA((10,)),
            pltpu.SemaphoreType.DMA((10,)),
            pltpu.SemaphoreType.DMA((12,)),
            pltpu.SemaphoreType.DMA((12,)),
            pltpu.SemaphoreType.DMA((12, 4)),
            pltpu.SemaphoreType.DMA((12, 4)),
            pltpu.SemaphoreType.DMA,
        ],
        compiler_params=pltpu.CompilerParams(
            collective_id=0, has_side_effects=True, vmem_limit_bytes=60 * 1024 * 1024
        ),
    )(units, meta, xm, xr, held)


def finish_kernel(yr, meta, held, place, state, live, am, ar, out, YM, YT, TM, TR):
    @pl.when(pl.program_id(0) == 0)
    def _():
        pos = [place[d] for d in range(3)]
        core = place[3]
        orders = [held[s] for s in range(SLOTS)]
        for j in range(3):
            for t in range(2):
                for e in range(2):
                    dest, dest_core = solver_coords(pos, core, j, t, e)
                    l = list_id(j, t, e)

                    def body(rc, carry):
                        TM[...] = yr[l, rc, 0:CHUNK, :].astype(F32)
                        tails = yr[l, rc, CHUNK:MSG, :].astype(F32)[0:PAIR_ROWS]
                        for u in range(8):
                            TR[PAIR_ROWS * u : PAIR_ROWS * (u + 1), :] = (
                                pltpu.roll(tails, 128 - 16 * u, 1) if u else tails
                            )
                        for u in range(8):
                            src = source_coords(dest, dest_core, j, rc, u // 2, u % 2)
                            low = meta[dest_core, src[2], src[1], src[0], 0, j]
                            for at, row in pair_rows(low, orders, TILE * TILES - 8):
                                put = PAIR_ROWS * u + at
                                YM[pl.ds(row, 2), :] = TM[put : put + 2, :]
                                YT[pl.ds(row, 2), :] = TR[put : put + 2, :]
                        return carry

                    lax.fori_loop(0, 4, body, 0)

    rows = pl.ds(pl.multiple_of(pl.program_id(0) * TILE, TILE), TILE)
    nt = (((1,), (1,)), ((), ()))
    lanes = lax.broadcasted_iota(jnp.int32, (TILE, 128), 1)
    tail = jnp.where(lanes < REM, YT[rows, :], 0.0).astype(BF16)
    total = lax.dot_general(am[...], YM[rows, :].astype(BF16), nt, preferred_element_type=F32)
    total += lax.dot_general(ar[...], tail, nt, preferred_element_type=F32)
    level = lax.broadcasted_iota(jnp.int32, total.shape, 0)
    total += jnp.where(level < LEV, 0.0, state[...].astype(F32))
    out[...] = jnp.where(live[...] > 0, total, 0.0).astype(BF16)


def finish(yr, meta, held, place, state, live, am, ar):
    smem = pl.BlockSpec(memory_space=pltpu.SMEM)
    rows = state.shape[0]
    block = pl.BlockSpec((rows, TILE), lambda i: (0, i))
    return pl.pallas_call(
        finish_kernel,
        grid=(TILES,),
        out_shape=jax.ShapeDtypeStruct(state.shape, BF16),
        in_specs=[
            pl.BlockSpec((12, 4, MSG, 128), lambda i: (0, 0, 0, 0)),
            smem,
            smem,
            smem,
            block,
            pl.BlockSpec((1, TILE), lambda i: (0, i)),
            pl.BlockSpec((rows, 128), lambda i: (0, 0)),
            pl.BlockSpec((rows, 128), lambda i: (0, 0)),
        ],
        out_specs=block,
        scratch_shapes=[
            pltpu.VMEM((TILE * TILES, 128), F32),
            pltpu.VMEM((TILE * TILES, 128), F32),
            pltpu.VMEM((CHUNK, 128), F32),
            pltpu.VMEM((CHUNK, 128), F32),
        ],
        compiler_params=pltpu.CompilerParams(vmem_limit_bytes=60 * 1024 * 1024),
    )(yr, meta, held, place, state, live, am, ar)


def unit_layout(inverses):
    turned = jnp.swapaxes(inverses, 2, 3)
    pad16 = ((0, 0), (0, 0), (0, 16 - REM), (0, 0))
    main = turned[:, :, :128, :128].reshape(3, 256, 128)
    bottom = jnp.pad(turned[:, :, 128:, :128], pad16).reshape(3, 32, 128)
    right = jnp.concatenate(
        [turned[:, :, :128, 128:].reshape(3, 256, REM), jnp.pad(turned[:, :, 128:, 128:], pad16).reshape(3, 32, REM)],
        axis=1,
    )
    groups = jnp.pad(right.reshape(3, 18, 16, REM), ((0, 0), (0, 2 * LANES14 - 18), (0, 0), (0, 0)))
    strips = groups.reshape(3, 2, LANES14, 16, REM).transpose(0, 1, 3, 2, 4).reshape(3, 32, LANES14 * REM)
    strips = jnp.pad(strips, ((0, 0), (0, 0), (0, 128 - LANES14 * REM)))
    return jnp.concatenate([main, bottom, strips], axis=1)


def shards(
    state,
    held_orders,
    pair_lows,
    inverses,
    height_operator,
    pressure_column,
    thermal_response_matrix,
    mass_row,
):
    denom = float(TRUNC * (TRUNC + 1))
    divergence = state[:LEV]
    thermal = state[LEV : 2 * LEV]
    pressure = state[2 * LEV]
    coeff = (jnp.arange(WIDTH, dtype=jnp.int32) // 2)[None, :]
    order_col = held_orders[:, None]
    degree = jnp.where(coeff <= TRUNC - order_col, order_col + coeff, coeff - 1)
    lap_scale = ((degree * (degree + 1)).astype(F32) / denom).reshape(-1)
    drive = lax.dot_general(thermal, height_operator, (((0,), (1,)), ((), ())), preferred_element_type=F32)
    drive = drive + pressure.astype(F32)[:, None] * pressure_column.astype(F32)[None, :]
    right_side = divergence.astype(F32).T + lap_scale[:, None] * drive
    xm = jnp.pad(right_side[:, :128], ((0, ROWS - COLS), (0, 0)))
    xr = jnp.pad(right_side[:, 128:], ((0, ROWS - COLS), (0, 128 - REM)))
    meta = jnp.zeros((1, 128), jnp.int32).at[0, 0:3].set(pair_lows).at[0, 8 : 8 + SLOTS].set(held_orders)
    yr, table = exchange(unit_layout(inverses), meta, xm, xr, held_orders)
    place = jnp.stack([lax.axis_index(name) for name in AXES]).astype(jnp.int32)
    live = jnp.repeat((held_orders >= 0).astype(F32), WIDTH)[None, :]
    operator = jnp.concatenate(
        [jnp.eye(LEV, dtype=BF16), -thermal_response_matrix, -mass_row[None, :]], axis=0
    )
    am = operator[:, :128]
    ar = jnp.pad(operator[:, 128:], ((0, 0), (0, 128 - REM)))
    return finish(yr, table, held_orders, place, state, live, am, ar)


def solution(mesh):
    torus = Mesh(mesh.devices.reshape(4, 4, 4, 2), AXES)
    columns = P(None, AXES)
    placed = (columns, P(AXES), P(AXES), P(AXES, None, None, None), P(), P(), P(), P())
    return jax.shard_map(shards, mesh=torus, in_specs=placed, out_specs=columns, check_vma=False)
```

time: 348 us -> 120 us (0.34); the launches traced: 343 us -> 119 us
  local copies, waits for them, and re-layouts: 191 us -> 18.2 us
  Pallas kernels: 0 us -> 85.2 us
  blocking collectives: 84.2 us -> 0 us
  waiting for transfers between devices: 32.9 us -> 0 us
  starting transfers between devices: 9.79 us -> 0 us
  matrix products: 10.8 us -> 6.89 us
  other arithmetic: 12.4 us -> 8.49 us
    pallas_call x0 -> x2, Pallas kernels: none -> 85.2 us  [the longest x1 65.9 us: exchange(): pl.pallas_call(exchange_kernel, out_shape=(jax.ShapeDtypeStruct((12, 4, M...]
    unnamed x36 -> x15, local copies, waits for them, and re-layouts: 57.9 us -> 4.14 us
    all_gather x4 -> x0, blocking collectives: 49.6 us -> none  [all_blocks(): tiles = lax.all_gather(tiles, axes[k], axis=0, tiled=True)]
    scatter x2, local copies, waits for them, and re-layouts: 49.1 us -> 0.88 us  [shards(): jnp.zeros((1, 128), jnp.int32).at[0, 0:3].set(pair_lows).at[0, 8:8 + SLOTS]]
    gather x3 -> x0, local copies, waits for them, and re-layouts: 44 us -> none  [shards(): message = jnp.take(right_side, column, axis=1, mode='fill', fill_value=0)]
    unnamed x2 -> x0, blocking collectives: 34.6 us -> none
    all_to_all x2 -> x0, waiting for transfers between devices: 32.9 us -> none  [the longest x1 32.9 us: send_home(): lax.all_to_all(message, GRP_WAVE, split_axis=1, concat_axis=1, tiled=True)]
    all_to_all x4 -> x0, local copies, waits for them, and re-layouts: 22.8 us -> none  [the longest x3 16.8 us: send_home(): lax.all_to_all(message, GRP_WAVE, split_axis=1, concat_axis=1, tiled=True)]
  transfers between devices with their start and end apart: 2 -> 0, of which waited for: 1 -> 0; matrix products, arithmetic and copies ran while one was open for 1% -> 0% of each run, Pallas kernels for 0% -> 0%
where the time goes in v1:
time: 120 us; the launch traced here: 119 us
  Pallas kernels  85.2 us (71%)
  local copies, waits for them, and re-layouts  18.2 us (15%)
  other arithmetic  8.49 us (7%)
  matrix products  6.89 us (6%)
    pallas_call x1, Pallas kernels, exchange(): pl.pallas_call(exchange_kernel, out_shape=(jax.ShapeDtypeStruct((12, 4, M...  65.9 us
    pallas_call x1, Pallas kernels, finish(): pl.pallas_call(finish_kernel, grid=(TILES,), out_shape=jax.ShapeDtypeStru...  19.3 us
    dot_general x1, matrix products, shards(): lax.dot_general(thermal, height_operator, (((0,), (1,)), ((), ())), prefe...  6.89 us
    another operation x5, other arithmetic  4.6 us
    unnamed x15, local copies, waits for them, and re-layouts  4.14 us

profile of v1, /device:TPU:1, one launch (start us, length us, event | category | flops | bytes accessed | tf_op | source)
XLA Modules:
  0.0 119.0 jit_solution(14412391019878078740)
XLA Ops:
  0.0 0.0 copy-start
  0.0 0.8 slice.84
  0.8 0.0 slice-start
  0.8 0.1 reshape.162
  0.9 0.9 slice.83
  1.9 0.2 reshape.155
  2.0 0.3 copy.26
  2.3 0.1 reshape.156
  2.4 0.8 copy.18
  3.2 0.3 reshape.157
  3.5 0.1 copy.19
  3.6 1.1 slice.81
  4.7 0.2 copy.13
  4.9 1.1 slice.82
  5.9 0.1 copy.25
  6.1 0.7 fusion.4.units_hbm
  6.8 0.6 slice.73
  7.4 0.6 compare_reduce_fusion
  8.1 1.3 %fusion.11 = s32[1,3]{1,0:T(1,128)S(1)} fusion(s32[3]{0:T(128)} %param.14, pred[]{:T(512)} %compare_reduce_fusion), kind=kLoop, calls=%fused_computation.29 | loop fusion | flops 3 | bytes 25 | tf_op jit(solution)/shard_map/reshape.61
  9.4 0.6 and_reduce_fusion
  10.0 2.0 %broadcast_select_fusion = s32[1,5]{1,0:T(1,128)S(1)} fusion(pred[]{:T(512)} %and_reduce_fusion, s32[5]{0:T(128)} %held.3, s32[]{:T(128)} %bitcast.6, s32[1,3]{1,0:T(1,128)S(1)} %fusion.11), kind=kLoop, calls=%fused_computation.27 | loop fusion | flops 5 | bytes 57 | tf_op jit(solution)/shard_map/select.3
  12.0 0.9 scatter.9.meta_hbm
  12.9 0.0 copy-start.3
  12.9 0.7 broadcast_subtract_fusion
  13.6 0.7 add_select_fusion
  14.3 0.1 select_n.29
  14.4 0.0 copy-start.4
  14.4 0.0 slice-done
  14.5 3.7 %copy.24 = bf16[137,7690]{0,1:T(8,128)(2,1)} copy(bf16[137,7690]{1,0:T(8,128)(2,1)S(1)} %slice-done) | data formatting | bytes 4214120
  18.2 0.0 copy-done.3
  18.2 1.0 convert_reduce_fusion
  19.2 0.0 copy-done.4
  19.2 0.0 copy-done
  19.2 6.9 %fusion.1 = f32[7690,137]{1,0:T(8,128)S(1)} fusion(bf16[137,137]{1,0:T(8,128)(2,1)S(1)} %copy-done, bf16[137,7690]{0,1:T(8,128)(2,1)} %copy.24, f32[137]{0:T(256)S(1)} %convert_element_type.44, f32[7690]{0:T(1024)S(1)} %convert_reduce_fusion, f32[7690]{0:T(1024)S(1)} %fusion.7, bf16[275,7690]{1,0:T(8,128)(2,1)} %state.1), kind=kOutput, calls=%fused_computation.2 | convolution fusion | flops 293934912 | bytes 10502782 | tf_op jit(solution)/shard_map/dot_general | solution.py:523
  26.1 0.3 slice.85
  26.4 2.2 %pad.40.xm_hbm = f32[7696,128]{1,0:T(8,128)} pad(f32[7690,128]{1,0:T(8,128)S(1)} %slice.85, f32[]{:T(128)} %constant.97.clone.1), padding=0_6x0_0 | pad | bytes 7877636 | tf_op jit(solution)/shard_map/jit(_pad)/pad | solution.py:526
  28.6 0.3 slice.86
  28.8 2.1 %pad.41.xr_hbm = f32[7696,128]{1,0:T(8,128)} pad(f32[7690,9]{1,0:T(8,128)S(1)} %slice.86, f32[]{:T(128)} %constant.97.clone.1), padding=0_6x0_119 | pad | bytes 4217196 | tf_op jit(solution)/shard_map/jit(_pad)/pad | solution.py:527
  31.0 65.9 %shard_map.82 = (bf16[12,4,224,128]{3,2,1,0:T(8,128)(2,1)}, s32[2,4,4,4,1,128]{5,4,3,2,1,0:T(1,128)}) custom-call(bf16[3,320,128]{2,1,0:T(8,128)(2,1)} %fusion.4.units_hbm, s32[1,128]{1,0:T(1,128)} %copy-done.3, f32[7696,128]{1,0:T(8,128)} %pad.40.xm_hbm, f32[7696,128]{1,0:T(8,128)} %pad.41.xr_hbm, s32[5]{0:T(128)} %held.3), custom_call_target="tpu_custom_call" | custom-call | tf_op jit(solution)/shard_map/pallas_call | solution.py:381
  96.9 0.7 pad_add_fusion.place
  97.6 0.0 copy-done.1
  97.6 0.0 copy-done.5
  97.7 0.7 pad.42.ar
  98.3 0.6 slice.87.am
  99.0 0.0 copy-done.2
  99.0 0.1 broadcast_in_dim.11
  99.1 0.7 broadcast_in_dim_reshape.4.live
  99.8 19.3 %shard_map.83 = bf16[275,7690]{1,0:T(8,128)(2,1)} custom-call(bf16[12,4,224,128]{3,2,1,0:T(8,128)(2,1)} %get-tuple-element.31.yr, s32[2,4,4,4,1,128]{5,4,3,2,1,0:T(1,128)} %get-tuple-element.32.meta, s32[5]{0:T(128)} %held.3, s32[4]{0:T(128)} %pad_add_fusion.place, bf16[275,7690]{1,0:T(8,128)(2,1)} %state.1, f32[1,7690]{1,0:T(1,128)} %broadcast_in_dim_reshape.4.live, ...), custom_call_target="tpu_custom_call" | custom-call | tf_op jit(solution)/shard_map/pallas_call | solution.py:465
  (22 shorter events, 0.3 us)
Async XLA Ops:
  0.0 19.2 %copy-start = (bf16[137,137]{1,0:T(8,128)(2,1)S(1)}, bf16[137,137]{1,0:T(8,128)(2,1)}, u32[]{:S(2)}) copy-start(bf16[137,137]{1,0:T(8,128)(2,1)} %param.16) | copy-start | bytes 112618
  0.8 13.7 %slice-start = ((bf16[275,7690]{1,0:T(8,128)(2,1)}), bf16[137,7690]{1,0:T(8,128)(2,1)S(1)}, s32[]{:S(2)}) async-start(bf16[275,7690]{1,0:T(8,128)(2,1)} %state.1), calls=%async_computation | async-start | bytes 4497408 | tf_op jit(solution)/shard_map/slice | solution.py:516
  12.9 5.3 %copy-start.3 = (s32[1,128]{1,0:T(1,128)}, s32[1,128]{1,0:T(1,128)S(1)}, u32[]{:S(2)}) copy-start(s32[1,128]{1,0:T(1,128)S(1)} %scatter.9.meta_hbm) | copy-start | bytes 1540
  14.4 4.8 %copy-start.4 = (bf16[137]{0:T(256)(128)(2,1)S(1)}, bf16[137]{0:T(256)(128)(2,1)}, u32[]{:S(2)}) copy-start(bf16[137]{0:T(256)(128)(2,1)} %param.17) | copy-start | bytes 826
  30.9 66.6 %copy-start.1 = (bf16[137,137]{1,0:T(8,128)(2,1)S(1)}, bf16[137,137]{1,0:T(8,128)(2,1)}, u32[]{:S(2)}) copy-start(bf16[137,137]{1,0:T(8,128)(2,1)} %param.18) | copy-start | bytes 112618
  30.9 66.7 %copy-start.5 = (bf16[137]{0:T(256)(128)(2,1)S(1)}, bf16[137]{0:T(256)(128)(2,1)}, u32[]{:S(2)}) copy-start(bf16[137]{0:T(256)(128)(2,1)} %param.19) | copy-start | bytes 826
  30.9 68.0 %copy-start.2 = (s32[5]{0:T(128)S(1)}, s32[5]{0:T(128)}, u32[]{:S(2)}) copy-start(s32[5]{0:T(128)} %held.3) | copy-start | bytes 64

commit v2 on v1

--- a/solution.py
+++ b/solution.py
@@ -19,12 +19,17 @@
 SLOTS = 5
 WIDTH = 2 * (TRUNC + 2)
 COLS = SLOTS * WIDTH
-ROWS = 7696
+ROWS = 8192
+MISS = ROWS - 8
 PAIR_ROWS = 24
 CHUNK = 8 * PAIR_ROWS
 MSG = 224
 UNIT = 320
-LANES14 = 14
+STRIP = 2 * REM
+PER_ROW = 7
+BLOCK = 768
+BLOCKS = 10
+TAIL_COLS = COLS - BLOCK * BLOCKS
 TILE = 1024
 TILES = 8
 
@@ -54,28 +59,18 @@
     return out
 
 
-def slot_rows(low, order):
-    first = jnp.where(order <= low, 2 * (low - order), 2 * (TRUNC + 1 - low))
-    second = 2 * (TRUNC - low - order)
-    return first, second
-
-
-def pair_rows(low, orders, miss):
-    rows = []
-    extra = miss
-    for s in range(SLOTS):
-        first, second = slot_rows(low, orders[s])
-        rows.append((2 * s, s * WIDTH + first))
-        rows.append((2 * SLOTS + 2 * s, s * WIDTH + second))
-        extra = jnp.where(orders[s] == low, s * WIDTH + 2 * (TRUNC + 1 - low), extra)
-    rows.append((4 * SLOTS, extra))
-    return rows
+def copy_items(table, line, u, target, source):
+    for t in range(2 * SLOTS + 1):
+        put = PAIR_ROWS * u + 2 * t
+        row = table[line, 16 * u + t]
+        for to, of in zip(target, source):
+            yield to, of, put, row
 
 
 def exchange_kernel(
-    units_hbm, meta_hbm, xm_hbm, xr_hbm, held,
-    yr_out, meta_out,
-    G, META, METAS, XM, XR, SND, RCV, YS, YR, TM, TR, MV, RA,
+    inv_hbm, state_hbm, drive_hbm, lows, held,
+    yr_out, table_out,
+    RAW, STATE, DRIVE, G, META, METAS, TABLE, TABLES, XM, XR, SND, RCV, YS, YR, TM, TR, MV, RA,
     in_sem, g_send, g_recv, m_send, m_recv, f_send, f_recv, b_send, b_recv, out_sem,
 ):
     pos = [lax.axis_index(AXES[d]) for d in range(3)]
@@ -87,12 +82,10 @@
     def shifted(d, delta):
         return [(pos[k] + 4 + delta) % 4 if k == d else pos[k] for k in range(3)]
 
-    own_meta = META.at[core, pos[2], pos[1], pos[0]]
     loads = [
-        pltpu.make_async_copy(units_hbm, G.at[:, 0, 0, 0], in_sem.at[0]),
-        pltpu.make_async_copy(meta_hbm, own_meta, in_sem.at[1]),
-        pltpu.make_async_copy(xm_hbm, XM, in_sem.at[2]),
-        pltpu.make_async_copy(xr_hbm, XR, in_sem.at[3]),
+        pltpu.make_async_copy(inv_hbm, RAW, in_sem.at[0]),
+        pltpu.make_async_copy(drive_hbm, DRIVE, in_sem.at[1]),
+        pltpu.make_async_copy(state_hbm, STATE, in_sem.at[2]),
     ]
     for load in loads:
         load.start()
@@ -107,6 +100,26 @@
     peers.append((pos, 1 - core))
     for coords, c in peers:
         pl.semaphore_signal(barrier, inc=1, device_id=device(coords, c), device_id_type=MESH)
+
+    lane1 = lax.broadcasted_iota(jnp.int32, (1, 128), 1)
+    record = jnp.zeros((1, 128), jnp.int32)
+    for k in range(3):
+        record = jnp.where(lane1 == k, lows[k], record)
+    for k in range(SLOTS):
+        record = jnp.where(lane1 == 8 + k, held[k], record)
+    META[core, pos[2], pos[1], pos[0]] = record
+    loads[0].wait()
+    for j in range(3):
+        strips = [jnp.zeros((16, 128), F32)] * 2
+        for h in range(2):
+            G[j, 0, 0, 0, 128 * h : 128 * (h + 1), :] = RAW[j, h, 0:128, 0:128]
+            G[j, 0, 0, 0, 256 + 16 * h : 272 + 16 * h, :] = RAW[j, h, 128:144, 0:128]
+            for g in range(9):
+                part = RAW[j, h, 16 * g : 16 * (g + 1), 128:256].astype(F32)
+                shift = STRIP * (g % PER_ROW) + REM * h
+                strips[g // PER_ROW] += pltpu.roll(part, shift, 1) if shift else part
+        for k in range(2):
+            G[j, 0, 0, 0, 288 + 16 * k : 304 + 16 * k, :] = strips[k].astype(BF16)
     pl.semaphore_wait(barrier, len(peers))
 
     def unit_copy(j, dest):
@@ -178,32 +191,101 @@
         for item in meta_copies(stage):
             meta_copy(*item).wait_recv()
 
-    loads[1].wait()
+    orders = [held[s] for s in range(SLOTS)]
+    eye = (
+        lax.broadcasted_iota(jnp.int32, (128, 128), 0) == lax.broadcasted_iota(jnp.int32, (128, 128), 1)
+    ).astype(BF16)
+    nt = (((1,), (1,)), ((), ()))
+
+    def turn(all_rows, base, width):
+        drive = jnp.dot(DRIVE[...], all_rows, preferred_element_type=F32)
+        col = base + lax.broadcasted_iota(jnp.int32, (1, width), 1)
+        order = jnp.full((1, width), orders[0], jnp.int32)
+        start = jnp.zeros((1, width), jnp.int32)
+        for s in range(1, SLOTS):
+            order = jnp.where(col >= s * WIDTH, orders[s], order)
+            start = jnp.where(col >= s * WIDTH, s * WIDTH, start)
+        q = (col - start) // 2
+        degree = jnp.where(q <= TRUNC - order, order + q, q - 1)
+        scale = (degree * (degree + 1)).astype(F32) / float(TRUNC * (TRUNC + 1))
+        level = lax.broadcasted_iota(jnp.int32, (144, width), 0)
+        divergence = jnp.where(level < LEV, all_rows[0:144].astype(F32), 0.0)
+        right = (divergence + scale * drive).astype(BF16)
+        for k in range(width // 128):
+            out = lax.dot_general(eye, right[:, 128 * k : 128 * (k + 1)], nt, preferred_element_type=F32)
+            rows = pl.ds(pl.multiple_of(base + 128 * k, 128), 128)
+            XM[rows, :] = out[:, 0:128]
+            XR[rows, 0:16] = out[:, 128:144]
+
+    def turn_blocks(first, last):
+        def body(i, carry):
+            base = pl.multiple_of(i * BLOCK, BLOCK)
+            turn(STATE[:, pl.ds(base, BLOCK)], base, BLOCK)
+            return carry
+
+        lax.fori_loop(first, last, body, 0)
+
     meta_start(0)
-    loads[0].wait()
     send((0, 0, 1), (0, 1, 0), (0, 3, 0), (1, 0, 0), (3, 0, 0))
     TM[...] = jnp.zeros_like(TM)
     TR[...] = jnp.zeros_like(TR)
+    XM[MISS - 504 : ROWS, :] = jnp.zeros((512, 128), F32)
+    XR[...] = jnp.zeros_like(XR)
+    loads[1].wait()
+    loads[2].wait()
+    turn_blocks(0, 2)
     meta_wait(0)
     meta_start(1)
+    send((0, 1, 1), (0, 3, 1), (1, 0, 1), (3, 0, 1))
+    turn_blocks(2, 5)
     meta_wait(1)
     meta_start(2)
+    send((0, 2, 0), (1, 1, 0), (3, 1, 0), (1, 3, 0), (3, 3, 0))
+    turn_blocks(5, 8)
     meta_wait(2)
     meta_start(3)
-    send((0, 1, 1), (0, 3, 1), (1, 0, 1), (3, 0, 1))
+    send((0, 2, 1), (1, 1, 1), (3, 1, 1), (1, 3, 1), (3, 3, 1))
+    turn_blocks(8, 10)
+    last = jnp.concatenate(
+        [STATE[:, BLOCK * BLOCKS : COLS], jnp.zeros((2 * LEV + 1, 128 - TAIL_COLS), BF16)], axis=1
+    )
+    turn(last, BLOCK * BLOCKS, 128)
     meta_wait(3)
-    table = pltpu.make_async_copy(META, METAS, in_sem.at[4])
-    table.start()
-    meta_store = pltpu.make_async_copy(META, meta_out, in_sem.at[5])
-    meta_store.start()
-    table.wait()
-    loads[2].wait()
-    loads[3].wait()
-
-    orders = [held[s] for s in range(SLOTS)]
+    send((2, 0, 0), (2, 0, 1))
+    fetch = pltpu.make_async_copy(META, METAS, in_sem.at[3])
+    fetch.start()
+    fetch.wait()
 
     def low_of(coords, c, j):
         return METAS[c, coords[2], coords[1], coords[0], 0, j]
+
+    every = [(t, e) for t in (1, 0) for e in (0, 1)]
+
+    for j in range(3):
+        for t, e in every:
+            dest, dest_core = solver_coords(pos, core, j, t, e)
+            for rc in range(4):
+                line = jnp.zeros((1, 128), jnp.int32)
+                for u in range(8):
+                    src = source_coords(dest, dest_core, j, rc, u // 2, u % 2)
+                    line = jnp.where(lane1 // 16 == u, low_of(src, dest_core, j), line)
+                at = 4 * list_id(j, t, e) + rc
+                TABLE[at : at + 1, :] = line
+    low = TABLE[...]
+    item = lax.broadcasted_iota(jnp.int32, (48, 128), 1) % 16
+    order = jnp.zeros((48, 128), jnp.int32)
+    extra = jnp.full((48, 128), MISS, jnp.int32)
+    for s in range(SLOTS):
+        order = jnp.where((item == s) | (item == SLOTS + s), orders[s], order)
+        extra = jnp.where(low == orders[s], s * WIDTH + 2 * (TRUNC + 1 - low), extra)
+    first = jnp.where(order <= low, 2 * (low - order), 2 * (TRUNC + 1 - low)) + item * WIDTH
+    second = 2 * (TRUNC - low - order) + (item - SLOTS) * WIDTH
+    TABLE[...] = jnp.where(item < SLOTS, first, jnp.where(item < 2 * SLOTS, second, extra))
+    table = pltpu.make_async_copy(TABLE, TABLES, in_sem.at[4])
+    table.start()
+    table_store = pltpu.make_async_copy(TABLE, table_out, in_sem.at[5])
+    table_store.start()
+    table.wait()
 
     def pack(j, t, e):
         dest, dest_core = solver_coords(pos, core, j, t, e)
@@ -212,12 +294,8 @@
 
         def body(rc, carry):
             for u in range(8):
-                src = source_coords(dest, dest_core, j, rc, u // 2, u % 2)
-                low = low_of(src, dest_core, j)
-                for at, row in pair_rows(low, orders, 0):
-                    put = PAIR_ROWS * u + at
-                    TM[put : put + 2, :] = XM[pl.ds(row, 2), :]
-                    TR[put : put + 2, :] = XR[pl.ds(row, 2), :]
+                for to, of, put, row in copy_items(TABLES, 4 * l + rc, u, (TM, TR), (XM, XR)):
+                    to[put : put + 2, :] = of[pl.ds(row, 2), :]
             target[l, rc, 0:CHUNK, :] = TM[...].astype(BF16)
             tail = TR[0:PAIR_ROWS, :]
             for u in range(1, 8):
@@ -252,7 +330,6 @@
             device_id=device(coords, c), device_id_type=MESH,
         )
 
-    every = [(t, e) for t in (1, 0) for e in (0, 1)]
     row_id = lax.broadcasted_iota(jnp.int32, (PAIR_ROWS, 128), 0)
 
     def order_rows(j):
@@ -284,27 +361,33 @@
                 is_low = MV[j] <= low
                 main = jnp.concatenate([jnp.where(is_low, x, 0.0), jnp.where(is_low, 0.0, x)], axis=1).astype(BF16)
                 tail_low = pltpu.roll(tails, (128 - 16 * u) % 128, 1)
-                tail_high = pltpu.roll(tails, (144 - 16 * u) % 128, 1)
+                tail_high = pltpu.roll(tails, (128 + REM - 16 * u) % 128, 1)
                 tail = jnp.where(
-                    lane < 16,
+                    lane < REM,
                     jnp.where(is_low, tail_low, 0.0),
-                    jnp.where(lane < 32, jnp.where(is_low, 0.0, tail_high), 0.0),
+                    jnp.where(lane < STRIP, jnp.where(is_low, 0.0, tail_high), 0.0),
                 ).astype(BF16)
                 strips = [unit[288:304, :].astype(F32), unit[304:320, :].astype(F32)]
                 strip = jnp.concatenate(
                     [
-                        pltpu.roll(strips[g // LANES14], (128 - REM * (g % LANES14)) % 128, 1)
-                        for g in range(18)
+                        pltpu.roll(strips[g // PER_ROW], (128 - STRIP * (g % PER_ROW)) % 128, 1)
+                        for g in range(9)
                     ],
                     axis=0,
                 ).astype(BF16)
-                weights = jnp.concatenate([unit[0:256, :], strip[0:256]], axis=1)
-                low_weights = jnp.concatenate([unit[256:288, :], strip[256:288]], axis=1)
-                y = jnp.dot(main, weights, preferred_element_type=F32) + jnp.dot(
-                    tail[:, 0:32], low_weights, preferred_element_type=F32
+                weights = jnp.concatenate(
+                    [
+                        jnp.concatenate([unit[0:128, :], unit[128:256, :]], axis=1),
+                        jnp.concatenate([unit[256:272, :], unit[272:288, :]], axis=1),
+                    ],
+                    axis=0,
+                )
+                y = lax.dot_general(main, weights, nt, preferred_element_type=F32) + lax.dot_general(
+                    tail, strip, nt, preferred_element_type=F32
                 )
                 solved.append(y[:, 0:128])
-                shifted_tail = pltpu.roll(y[:, 128:256], 16 * u, 1)
+                wide = jnp.concatenate([y[:, 128:144], jnp.zeros((4 * PAIR_ROWS, 112), F32)], axis=1)
+                shifted_tail = pltpu.roll(wide, 16 * u, 1)
                 keep = (lane >= 16 * u) & (lane < 16 * u + REM)
                 RA[...] += jnp.where(keep, shifted_tail, 0.0)
             for k in range(4):
@@ -330,19 +413,13 @@
     for j in range(3):
         pack(j, 1, 0)
         pack(j, 1, 1)
-        if j == 0:
-            send((0, 2, 0), (1, 1, 0), (3, 1, 0), (1, 3, 0), (3, 3, 0))
-        elif j == 1:
-            send((0, 2, 1), (1, 1, 1), (3, 1, 1), (1, 3, 1), (3, 3, 1))
-        else:
-            send((2, 0, 0), (2, 0, 1))
+    send((1, 2, 0), (3, 2, 0), (1, 2, 1), (3, 2, 1))
     for j in range(3):
         pack(j, 0, 1)
-    send((1, 2, 0), (3, 2, 0), (1, 2, 1), (3, 2, 1))
+    send((2, 1, 0), (2, 1, 1), (2, 3, 0), (2, 3, 1))
     for j in range(3):
         pack(j, 0, 0)
         order_rows(j)
-    send((2, 1, 0), (2, 1, 1), (2, 3, 0), (2, 3, 1))
 
     got = set()
 
@@ -362,34 +439,43 @@
     for rc in (1, 3, 2):
         for j in range(3):
             solve_ready(j, rc)
-    for j in range(3):
-        for rc in range(4):
-            for t, e in every:
+    stores = []
+    for j in range(3):
+        for t, e in every:
+            for rc in range(4):
                 if t + e:
                     return_copy(j, t, e, rc).wait_recv()
-    done = pltpu.make_async_copy(YR, yr_out, out_sem)
-    done.start()
-    done.wait()
-    meta_store.wait()
+            l = list_id(j, t, e)
+            stores.append(pltpu.make_async_copy(YR.at[l], yr_out.at[l], out_sem.at[l]))
+            stores[-1].start()
+    for store in stores:
+        store.wait()
+    table_store.wait()
     for copy in sent:
         copy.wait_send()
 
 
-def exchange(units, meta, xm, xr, held):
+def exchange(inverses, state, drive, lows, held):
     any_space = pl.BlockSpec(memory_space=pl.ANY)
+    smem = pl.BlockSpec(memory_space=pltpu.SMEM)
     messages = pltpu.VMEM((12, 4, MSG, 128), BF16)
     return pl.pallas_call(
         exchange_kernel,
         out_shape=(
             jax.ShapeDtypeStruct((12, 4, MSG, 128), BF16),
-            jax.ShapeDtypeStruct((2, 4, 4, 4, 1, 128), jnp.int32),
+            jax.ShapeDtypeStruct((48, 128), jnp.int32),
         ),
-        in_specs=[any_space] * 4 + [pl.BlockSpec(memory_space=pltpu.SMEM)],
+        in_specs=[any_space] * 3 + [smem, smem],
         out_specs=(any_space, any_space),
         scratch_shapes=[
+            pltpu.VMEM(inverses.shape, BF16),
+            pltpu.VMEM(state.shape, BF16),
+            pltpu.VMEM(drive.shape, BF16),
             pltpu.VMEM((3, 4, 4, 2, UNIT, 128), BF16),
             pltpu.VMEM((2, 4, 4, 4, 1, 128), jnp.int32),
             pltpu.SMEM((2, 4, 4, 4, 1, 128), jnp.int32),
+            pltpu.VMEM((48, 128), jnp.int32),
+            pltpu.SMEM((48, 128), jnp.int32),
             pltpu.VMEM((ROWS, 128), F32),
             pltpu.VMEM((ROWS, 128), F32),
             messages,
@@ -409,56 +495,46 @@
             pltpu.SemaphoreType.DMA((12,)),
             pltpu.SemaphoreType.DMA((12, 4)),
             pltpu.SemaphoreType.DMA((12, 4)),
-            pltpu.SemaphoreType.DMA,
+            pltpu.SemaphoreType.DMA((12,)),
         ],
         compiler_params=pltpu.CompilerParams(
             collective_id=0, has_side_effects=True, vmem_limit_bytes=60 * 1024 * 1024
         ),
-    )(units, meta, xm, xr, held)
-
-
-def finish_kernel(yr, meta, held, place, state, live, am, ar, out, YM, YT, TM, TR):
+    )(inverses, state, drive, lows, held)
+
+
+def finish_kernel(yr, table, held, state, operator, out, YM, YT, TM, TR):
     @pl.when(pl.program_id(0) == 0)
     def _():
-        pos = [place[d] for d in range(3)]
-        core = place[3]
-        orders = [held[s] for s in range(SLOTS)]
-        for j in range(3):
-            for t in range(2):
-                for e in range(2):
-                    dest, dest_core = solver_coords(pos, core, j, t, e)
-                    l = list_id(j, t, e)
-
-                    def body(rc, carry):
-                        TM[...] = yr[l, rc, 0:CHUNK, :].astype(F32)
-                        tails = yr[l, rc, CHUNK:MSG, :].astype(F32)[0:PAIR_ROWS]
-                        for u in range(8):
-                            TR[PAIR_ROWS * u : PAIR_ROWS * (u + 1), :] = (
-                                pltpu.roll(tails, 128 - 16 * u, 1) if u else tails
-                            )
-                        for u in range(8):
-                            src = source_coords(dest, dest_core, j, rc, u // 2, u % 2)
-                            low = meta[dest_core, src[2], src[1], src[0], 0, j]
-                            for at, row in pair_rows(low, orders, TILE * TILES - 8):
-                                put = PAIR_ROWS * u + at
-                                YM[pl.ds(row, 2), :] = TM[put : put + 2, :]
-                                YT[pl.ds(row, 2), :] = TR[put : put + 2, :]
-                        return carry
-
-                    lax.fori_loop(0, 4, body, 0)
+        def body(line, carry):
+            l, rc = line // 4, line % 4
+            TM[...] = yr[l, rc, 0:CHUNK, :].astype(F32)
+            tails = yr[l, rc, CHUNK:MSG, :].astype(F32)[0:PAIR_ROWS]
+            for u in range(8):
+                TR[PAIR_ROWS * u : PAIR_ROWS * (u + 1), :] = pltpu.roll(tails, 128 - 16 * u, 1) if u else tails
+            for u in range(8):
+                for to, of, put, row in copy_items(table, line, u, (YM, YT), (TM, TR)):
+                    to[pl.ds(row, 2), :] = of[put : put + 2, :]
+            return carry
+
+        lax.fori_loop(0, 48, body, 0)
 
     rows = pl.ds(pl.multiple_of(pl.program_id(0) * TILE, TILE), TILE)
     nt = (((1,), (1,)), ((), ()))
     lanes = lax.broadcasted_iota(jnp.int32, (TILE, 128), 1)
     tail = jnp.where(lanes < REM, YT[rows, :], 0.0).astype(BF16)
-    total = lax.dot_general(am[...], YM[rows, :].astype(BF16), nt, preferred_element_type=F32)
-    total += lax.dot_general(ar[...], tail, nt, preferred_element_type=F32)
+    total = lax.dot_general(operator[:, 0:128], YM[rows, :].astype(BF16), nt, preferred_element_type=F32)
+    total += lax.dot_general(operator[:, 128:256], tail, nt, preferred_element_type=F32)
     level = lax.broadcasted_iota(jnp.int32, total.shape, 0)
     total += jnp.where(level < LEV, 0.0, state[...].astype(F32))
-    out[...] = jnp.where(live[...] > 0, total, 0.0).astype(BF16)
-
-
-def finish(yr, meta, held, place, state, live, am, ar):
+    col = pl.program_id(0) * TILE + lax.broadcasted_iota(jnp.int32, (1, TILE), 1)
+    order = jnp.full((1, TILE), held[0], jnp.int32)
+    for s in range(1, SLOTS):
+        order = jnp.where(col >= s * WIDTH, held[s], order)
+    out[...] = jnp.where(order >= 0, total, 0.0).astype(BF16)
+
+
+def finish(yr, table, held, state, operator):
     smem = pl.BlockSpec(memory_space=pltpu.SMEM)
     rows = state.shape[0]
     block = pl.BlockSpec((rows, TILE), lambda i: (0, i))
@@ -470,11 +546,8 @@
             pl.BlockSpec((12, 4, MSG, 128), lambda i: (0, 0, 0, 0)),
             smem,
             smem,
-            smem,
             block,
-            pl.BlockSpec((1, TILE), lambda i: (0, i)),
-            pl.BlockSpec((rows, 128), lambda i: (0, 0)),
-            pl.BlockSpec((rows, 128), lambda i: (0, 0)),
+            pl.BlockSpec((rows, 256), lambda i: (0, 0)),
         ],
         out_specs=block,
         scratch_shapes=[
@@ -484,22 +557,7 @@
             pltpu.VMEM((CHUNK, 128), F32),
         ],
         compiler_params=pltpu.CompilerParams(vmem_limit_bytes=60 * 1024 * 1024),
-    )(yr, meta, held, place, state, live, am, ar)
-
-
-def unit_layout(inverses):
-    turned = jnp.swapaxes(inverses, 2, 3)
-    pad16 = ((0, 0), (0, 0), (0, 16 - REM), (0, 0))
-    main = turned[:, :, :128, :128].reshape(3, 256, 128)
-    bottom = jnp.pad(turned[:, :, 128:, :128], pad16).reshape(3, 32, 128)
-    right = jnp.concatenate(
-        [turned[:, :, :128, 128:].reshape(3, 256, REM), jnp.pad(turned[:, :, 128:, 128:], pad16).reshape(3, 32, REM)],
-        axis=1,
-    )
-    groups = jnp.pad(right.reshape(3, 18, 16, REM), ((0, 0), (0, 2 * LANES14 - 18), (0, 0), (0, 0)))
-    strips = groups.reshape(3, 2, LANES14, 16, REM).transpose(0, 1, 3, 2, 4).reshape(3, 32, LANES14 * REM)
-    strips = jnp.pad(strips, ((0, 0), (0, 0), (0, 128 - LANES14 * REM)))
-    return jnp.concatenate([main, bottom, strips], axis=1)
+    )(yr, table, held, state, operator)
 
 
 def shards(
@@ -512,29 +570,13 @@
     thermal_response_matrix,
     mass_row,
 ):
-    denom = float(TRUNC * (TRUNC + 1))
-    divergence = state[:LEV]
-    thermal = state[LEV : 2 * LEV]
-    pressure = state[2 * LEV]
-    coeff = (jnp.arange(WIDTH, dtype=jnp.int32) // 2)[None, :]
-    order_col = held_orders[:, None]
-    degree = jnp.where(coeff <= TRUNC - order_col, order_col + coeff, coeff - 1)
-    lap_scale = ((degree * (degree + 1)).astype(F32) / denom).reshape(-1)
-    drive = lax.dot_general(thermal, height_operator, (((0,), (1,)), ((), ())), preferred_element_type=F32)
-    drive = drive + pressure.astype(F32)[:, None] * pressure_column.astype(F32)[None, :]
-    right_side = divergence.astype(F32).T + lap_scale[:, None] * drive
-    xm = jnp.pad(right_side[:, :128], ((0, ROWS - COLS), (0, 0)))
-    xr = jnp.pad(right_side[:, 128:], ((0, ROWS - COLS), (0, 128 - REM)))
-    meta = jnp.zeros((1, 128), jnp.int32).at[0, 0:3].set(pair_lows).at[0, 8 : 8 + SLOTS].set(held_orders)
-    yr, table = exchange(unit_layout(inverses), meta, xm, xr, held_orders)
-    place = jnp.stack([lax.axis_index(name) for name in AXES]).astype(jnp.int32)
-    live = jnp.repeat((held_orders >= 0).astype(F32), WIDTH)[None, :]
-    operator = jnp.concatenate(
-        [jnp.eye(LEV, dtype=BF16), -thermal_response_matrix, -mass_row[None, :]], axis=0
-    )
-    am = operator[:, :128]
-    ar = jnp.pad(operator[:, 128:], ((0, 0), (0, 128 - REM)))
-    return finish(yr, table, held_orders, place, state, live, am, ar)
+    padded = jnp.pad(inverses, ((0, 0), (0, 0), (0, 144 - LEV), (0, 256 - LEV)))
+    drive = jnp.concatenate([jnp.zeros((LEV, LEV), BF16), height_operator, pressure_column[:, None]], axis=1)
+    drive = jnp.pad(drive, ((0, 144 - LEV), (0, 0)))
+    yr, table = exchange(padded, state, drive, pair_lows, held_orders)
+    operator = jnp.concatenate([jnp.eye(LEV, dtype=BF16), -thermal_response_matrix, -mass_row[None, :]], axis=0)
+    operator = jnp.pad(operator, ((0, 0), (0, 256 - LEV)))
+    return finish(yr, table, held_orders, state, operator)
 
 
 def solution(mesh):

time: 120 us -> 86.3 us (0.72)
  local copies, waits for them, and re-layouts: 18.2 us -> 3.31 us
  matrix products: 6.89 us -> 0 us
  Pallas kernels: 85.2 us -> 79.3 us
  other arithmetic: 8.49 us -> 3.27 us
    dot_general x1 -> x0, matrix products: 6.89 us -> none  [shards(): lax.dot_general(thermal, height_operator, (((0,), (1,)), ((), ())), prefe...]
    another operation x6 -> x0, other arithmetic: 5.25 us -> none
    slice x12 -> x0, local copies, waits for them, and re-layouts: 5.1 us -> none  [the longest x2 1.25 us: unit_layout(): main = turned[:, :, :128, :128].reshape(3, 256, 128)]
    pallas_call x1, Pallas kernels: 65.9 us -> 61.8 us  [exchange(): pl.pallas_call(exchange_kernel, out_shape=(jax.ShapeDtypeStruct((12, 4, M...]
    pad x6 -> x2, local copies, waits for them, and re-layouts: 5.02 us -> 1.49 us  [the longest x1 0.84 us: shards(): padded = jnp.pad(inverses, ((0, 0), (0, 0), (0, 144 - LEV), (0, 256 - LEV)))]
    unnamed x15 -> x1, local copies, waits for them, and re-layouts: 4.14 us -> 1.06 us
    pallas_call x1, Pallas kernels: 19.3 us -> 17.4 us  [finish(): pl.pallas_call(finish_kernel, grid=(TILES,), out_shape=jax.ShapeDtypeStru...]
    another operation x2 -> x0, local copies, waits for them, and re-layouts: 1.33 us -> none  [the longest x1 0.72 us: shards(): live = jnp.repeat((held_orders >= 0).astype(F32), WIDTH)[None, :]]
where the time goes in v2:
time: 86.3 us; the launch traced here: 85.9 us
  Pallas kernels  79.3 us (92%)
  local copies, waits for them, and re-layouts  3.31 us (4%)
  other arithmetic  3.27 us (4%)
    pallas_call x1, Pallas kernels, exchange(): pl.pallas_call(exchange_kernel, out_shape=(jax.ShapeDtypeStruct((12, 4, M...  61.8 us
    pallas_call x1, Pallas kernels, finish(): pl.pallas_call(finish_kernel, grid=(TILES,), out_shape=jax.ShapeDtypeStru...  17.4 us

profile of v2, /device:TPU:1, one launch (start us, length us, event | category | flops | bytes accessed | tf_op | source)
XLA Modules:
  0.0 85.9 jit_solution(1673126186881530440)
XLA Ops:
  0.0 0.7 neg.10
  0.7 0.7 broadcast_in_dim.9
  1.4 1.0 %pad_maximum_fusion = bf16[137,275]{1,0:T(8,128)(2,1)S(1)} fusion(bf16[137,1]{1,0:T(8,128)(2,1)S(1)} %broadcast_in_dim.9, bf16[137,137]{1,0:T(8,128)(2,1)} %param.12, bf16[275]{0:T(512)(128)(2,1)S(1)} %pad.18.clone), kind=kLoop, calls=%fused_computation.8 | loop fusion | flops 226050 | bytes 113712 | tf_op jit(solution)/shard_map/concatenate | solution.py:574
  2.4 0.7 pad.13.drive_hbm
  3.1 0.9 %neg.9 = bf16[137,137]{1,0:T(8,128)(2,1)S(1)} negate(bf16[137,137]{1,0:T(8,128)(2,1)} %param.14) | non-fusion elementwise | flops 18769 | bytes 75076 | tf_op jit(solution)/shard_map/neg | solution.py:577
  4.0 0.7 fusion.5.operator
  4.7 1.1 %copy.10 = bf16[3,2,137,137]{3,2,1,0:T(8,128)(2,1)S(1)} copy(bf16[3,2,137,137]{3,1,2,0:T(2,128)(2,1)} %param.11) | data formatting | bytes 450456 | tf_op args[3]
  5.8 0.8 pad.12.inv_hbm
  6.6 61.8 %shard_map.82 = (bf16[12,4,224,128]{3,2,1,0:T(8,128)(2,1)}, s32[48,128]{1,0:T(8,128)}) custom-call(bf16[3,2,144,256]{3,2,1,0:T(8,128)(2,1)} %pad.12.inv_hbm, bf16[275,7690]{1,0:T(8,128)(2,1)} %state.1, bf16[144,275]{1,0:T(8,128)(2,1)} %pad.13.drive_hbm, s32[3]{0:T(128)} %lows.1, s32[5]{0:T(128)} %held.3), custom_call_target="tpu_custom_call" | custom-call | tf_op jit(solution)/shard_map/pallas_call | solution.py:462
  68.5 17.4 %shard_map.83 = bf16[275,7690]{1,0:T(8,128)(2,1)} custom-call(bf16[12,4,224,128]{3,2,1,0:T(8,128)(2,1)} %get-tuple-element.7.yr, s32[48,128]{1,0:T(8,128)} %get-tuple-element.8.table, s32[5]{0:T(128)} %held.3, bf16[275,7690]{1,0:T(8,128)(2,1)} %state.1, bf16[275,256]{1,0:T(8,128)(2,1)} %fusion.5.operator), custom_call_target="tpu_custom_call" | custom-call | tf_op jit(solution)/shard_map/pallas_call | solution.py:541
  (4 shorter events, 0.0 us)

commit v3 on v2

--- a/solution.py
+++ b/solution.py
@@ -68,9 +68,9 @@
 
 
 def exchange_kernel(
-    inv_hbm, state_hbm, drive_hbm, lows, held,
+    inv_hbm, state_hbm, height, pressure, lows, held,
     yr_out, table_out,
-    RAW, STATE, DRIVE, G, META, METAS, TABLE, TABLES, XM, XR, SND, RCV, YS, YR, TM, TR, MV, RA,
+    RAW, STATE, DRIVE, G, META, METAS, TABLE, TABLES, XM, XR, SND, RCV, YS, YR, TM, TR, MV,
     in_sem, g_send, g_recv, m_send, m_recv, f_send, f_recv, b_send, b_recv, out_sem,
 ):
     pos = [lax.axis_index(AXES[d]) for d in range(3)]
@@ -84,20 +84,21 @@
 
     loads = [
         pltpu.make_async_copy(inv_hbm, RAW, in_sem.at[0]),
-        pltpu.make_async_copy(drive_hbm, DRIVE, in_sem.at[1]),
-        pltpu.make_async_copy(state_hbm, STATE, in_sem.at[2]),
+        pltpu.make_async_copy(state_hbm, STATE, in_sem.at[1]),
     ]
     for load in loads:
         load.start()
 
     barrier = pltpu.get_barrier_semaphore()
-    peers = []
+    other = 1 - core
+    peers = [(pos, other)]
     for d in range(3):
         for delta in (1, -1):
             peers.append((shifted(d, delta), core))
-            peers.append((shifted(d, delta), 1 - core))
+            peers.append((shifted(d, delta), other))
         peers.append((shifted(d, 2), core))
-    peers.append((pos, 1 - core))
+    peers.append((shifted(0, 2), other))
+
     for coords, c in peers:
         pl.semaphore_signal(barrier, inc=1, device_id=device(coords, c), device_id_type=MESH)
 
@@ -107,15 +108,27 @@
         record = jnp.where(lane1 == k, lows[k], record)
     for k in range(SLOTS):
         record = jnp.where(lane1 == 8 + k, held[k], record)
-    META[core, pos[2], pos[1], pos[0]] = record
+    META[pos[2], pos[1], core, pos[0]] = record
+
+    def chosen(rows, cols, test):
+        r = lax.broadcasted_iota(jnp.int32, (rows, cols), 0)
+        c = lax.broadcasted_iota(jnp.int32, (rows, cols), 1)
+        return test(r, c).astype(BF16)
+
+    below = chosen(16, LEV, lambda r, c: c == r + 128)
+    beside = chosen(LEV, 128, lambda r, c: r == c + 128)
     loads[0].wait()
     for j in range(3):
         strips = [jnp.zeros((16, 128), F32)] * 2
         for h in range(2):
-            G[j, 0, 0, 0, 128 * h : 128 * (h + 1), :] = RAW[j, h, 0:128, 0:128]
-            G[j, 0, 0, 0, 256 + 16 * h : 272 + 16 * h, :] = RAW[j, h, 128:144, 0:128]
+            raw = RAW[j, :, h, :]
+            bottom = jnp.dot(below, raw, preferred_element_type=F32).astype(BF16)
+            right = jnp.dot(raw, beside, preferred_element_type=F32)
+            corner = jnp.dot(bottom, beside, preferred_element_type=F32)
+            G[j, 0, 0, 0, 128 * h : 128 * (h + 1), :] = raw[0:128, 0:128]
+            G[j, 0, 0, 0, 256 + 16 * h : 272 + 16 * h, :] = bottom[:, 0:128]
             for g in range(9):
-                part = RAW[j, h, 16 * g : 16 * (g + 1), 128:256].astype(F32)
+                part = right[16 * g : 16 * (g + 1)] if g < 8 else corner
                 shift = STRIP * (g % PER_ROW) + REM * h
                 strips[g // PER_ROW] += pltpu.roll(part, shift, 1) if shift else part
         for k in range(2):
@@ -164,15 +177,12 @@
                 sent.append(copy)
 
     def meta_copies(stage):
-        out = []
-        if stage < 3:
-            d = stage
-            index = (core, pos[2], pos[1], pos[0])[: 4 - d]
-            for delta in (1, 2, 3):
-                out.append((index, device(shifted(d, delta), core), 3 * d + delta - 1))
-        else:
-            out.append(((core,), device(pos, 1 - core), 9))
-        return out
+        if stage == 0:
+            index = (pos[2], pos[1], core, pos[0])
+            out = [(index, device(shifted(0, delta), core), delta - 1) for delta in (1, 2, 3)]
+            return out + [(index, device(shifted(0, delta), other), 3 + delta) for delta in range(4)]
+        index = (pos[2], pos[1])[: 3 - stage]
+        return [(index, device(shifted(stage, delta), core), 3 + 3 * stage + delta) for delta in (1, 2, 3)]
 
     def meta_copy(index, dev, sem):
         ref = META.at[index]
@@ -198,7 +208,7 @@
     nt = (((1,), (1,)), ((), ()))
 
     def turn(all_rows, base, width):
-        drive = jnp.dot(DRIVE[...], all_rows, preferred_element_type=F32)
+        drive = jnp.dot(DRIVE[0:144, :], all_rows, preferred_element_type=F32)
         col = base + lax.broadcasted_iota(jnp.int32, (1, width), 1)
         order = jnp.full((1, width), orders[0], jnp.int32)
         start = jnp.zeros((1, width), jnp.int32)
@@ -231,33 +241,33 @@
     TR[...] = jnp.zeros_like(TR)
     XM[MISS - 504 : ROWS, :] = jnp.zeros((512, 128), F32)
     XR[...] = jnp.zeros_like(XR)
+    rows = 2 * LEV + 1
+    diagonal = chosen(LEV, LEV, lambda r, c: r == c) * jnp.broadcast_to(pressure[...][None, :], (LEV, LEV))
+    thermal_rows = chosen(LEV, rows, lambda r, c: c == r + LEV)
+    pressure_row = chosen(LEV, rows, lambda r, c: c == 2 * LEV)
+    DRIVE[...] = jnp.zeros_like(DRIVE)
+    DRIVE[0:LEV, :] = (
+        jnp.dot(height[...], thermal_rows, preferred_element_type=F32)
+        + jnp.dot(diagonal, pressure_row, preferred_element_type=F32)
+    ).astype(BF16)
     loads[1].wait()
-    loads[2].wait()
-    turn_blocks(0, 2)
+    turn_blocks(0, 7)
     meta_wait(0)
     meta_start(1)
     send((0, 1, 1), (0, 3, 1), (1, 0, 1), (3, 0, 1))
-    turn_blocks(2, 5)
+    turn_blocks(7, 10)
+    last = jnp.concatenate([STATE[:, BLOCK * BLOCKS : COLS], jnp.zeros((rows, 128 - TAIL_COLS), BF16)], axis=1)
+    turn(last, BLOCK * BLOCKS, 128)
     meta_wait(1)
     meta_start(2)
     send((0, 2, 0), (1, 1, 0), (3, 1, 0), (1, 3, 0), (3, 3, 0))
-    turn_blocks(5, 8)
+    send((0, 2, 1), (1, 1, 1), (3, 1, 1), (1, 3, 1), (3, 3, 1))
     meta_wait(2)
-    meta_start(3)
-    send((0, 2, 1), (1, 1, 1), (3, 1, 1), (1, 3, 1), (3, 3, 1))
-    turn_blocks(8, 10)
-    last = jnp.concatenate(
-        [STATE[:, BLOCK * BLOCKS : COLS], jnp.zeros((2 * LEV + 1, 128 - TAIL_COLS), BF16)], axis=1
-    )
-    turn(last, BLOCK * BLOCKS, 128)
-    meta_wait(3)
-    send((2, 0, 0), (2, 0, 1))
-    fetch = pltpu.make_async_copy(META, METAS, in_sem.at[3])
+    fetch = pltpu.make_async_copy(META, METAS, in_sem.at[2])
     fetch.start()
-    fetch.wait()
 
     def low_of(coords, c, j):
-        return METAS[c, coords[2], coords[1], coords[0], 0, j]
+        return METAS[coords[2], coords[1], c, coords[0], 0, j]
 
     every = [(t, e) for t in (1, 0) for e in (0, 1)]
 
@@ -268,7 +278,8 @@
                 line = jnp.zeros((1, 128), jnp.int32)
                 for u in range(8):
                     src = source_coords(dest, dest_core, j, rc, u // 2, u % 2)
-                    line = jnp.where(lane1 // 16 == u, low_of(src, dest_core, j), line)
+                    entry = META[src[2], src[1], dest_core, src[0]]
+                    line = jnp.where(lane1 // 16 == u, jnp.broadcast_to(entry[:, j : j + 1], (1, 128)), line)
                 at = 4 * list_id(j, t, e) + rc
                 TABLE[at : at + 1, :] = line
     low = TABLE[...]
@@ -281,10 +292,11 @@
     first = jnp.where(order <= low, 2 * (low - order), 2 * (TRUNC + 1 - low)) + item * WIDTH
     second = 2 * (TRUNC - low - order) + (item - SLOTS) * WIDTH
     TABLE[...] = jnp.where(item < SLOTS, first, jnp.where(item < 2 * SLOTS, second, extra))
-    table = pltpu.make_async_copy(TABLE, TABLES, in_sem.at[4])
+    table = pltpu.make_async_copy(TABLE, TABLES, in_sem.at[3])
     table.start()
-    table_store = pltpu.make_async_copy(TABLE, table_out, in_sem.at[5])
+    table_store = pltpu.make_async_copy(TABLE, table_out, in_sem.at[4])
     table_store.start()
+    send((2, 0, 0), (2, 0, 1))
     table.wait()
 
     def pack(j, t, e):
@@ -292,19 +304,17 @@
         l = list_id(j, t, e)
         target = RCV if t + e == 0 else SND
 
-        def body(rc, carry):
+        for rc in range(4):
             for u in range(8):
-                for to, of, put, row in copy_items(TABLES, 4 * l + rc, u, (TM, TR), (XM, XR)):
+                for to, of, put, row in copy_items(TABLES, 4 * l + rc, u, (TM.at[rc], TR.at[rc]), (XM, XR)):
                     to[put : put + 2, :] = of[pl.ds(row, 2), :]
-            target[l, rc, 0:CHUNK, :] = TM[...].astype(BF16)
-            tail = TR[0:PAIR_ROWS, :]
+            target[l, rc, 0:CHUNK, :] = TM[rc].astype(BF16)
+            tail = TR[rc, 0:PAIR_ROWS, :]
             for u in range(1, 8):
-                tail += pltpu.roll(TR[PAIR_ROWS * u : PAIR_ROWS * (u + 1), :], 16 * u, 1)
+                tail += pltpu.roll(TR[rc, PAIR_ROWS * u : PAIR_ROWS * (u + 1), :], 16 * u, 1)
             tail = jnp.concatenate([tail, jnp.zeros((MSG - CHUNK - PAIR_ROWS, 128), F32)], axis=0)
             target[l, rc, CHUNK:MSG, :] = tail.astype(BF16)
-            return carry
-
-        lax.fori_loop(0, 4, body, 0)
+
         if t + e:
             copy = forward_copy(j, t, e)
             copy.start()
@@ -337,21 +347,20 @@
             coords, c = origin(j, t, e)
             rows = jnp.full((PAIR_ROWS, 128), HALF + 1, jnp.int32)
             for s in range(SLOTS):
-                order = METAS[c, coords[2], coords[1], coords[0], 0, 8 + s]
+                order = METAS[coords[2], coords[1], c, coords[0], 0, 8 + s]
                 rows = jnp.where(row_id // 2 == s, order, rows)
             MV[j, PAIR_ROWS * (2 * t + e) : PAIR_ROWS * (2 * t + e + 1), :] = rows
 
     lane = lax.broadcasted_iota(jnp.int32, (4 * PAIR_ROWS, 128), 1)
 
     def solve(j, rc):
-        RA[...] = jnp.zeros_like(RA)
-
-        def body(rb, carry):
-            rows = pl.ds(pl.multiple_of(2 * PAIR_ROWS * rb, 16), 2 * PAIR_ROWS)
+        tails = jnp.concatenate(
+            [RCV[list_id(j, k // 2, k % 2), rc, CHUNK:MSG, :].astype(F32)[:PAIR_ROWS] for k in range(4)], axis=0
+        )
+        spread = jnp.zeros((4 * PAIR_ROWS, 128), F32)
+        for rb in range(4):
+            rows = slice(2 * PAIR_ROWS * rb, 2 * PAIR_ROWS * (rb + 1))
             mains = [RCV[list_id(j, k // 2, k % 2), rc, rows, :].astype(F32) for k in range(4)]
-            tails = jnp.concatenate(
-                [RCV[list_id(j, k // 2, k % 2), rc, CHUNK:MSG, :].astype(F32)[:PAIR_ROWS] for k in range(4)], axis=0
-            )
             solved = []
             for ra in range(2):
                 u = 2 * rb + ra
@@ -360,7 +369,7 @@
                 x = jnp.concatenate([m[PAIR_ROWS * ra : PAIR_ROWS * (ra + 1)] for m in mains], axis=0)
                 is_low = MV[j] <= low
                 main = jnp.concatenate([jnp.where(is_low, x, 0.0), jnp.where(is_low, 0.0, x)], axis=1).astype(BF16)
-                tail_low = pltpu.roll(tails, (128 - 16 * u) % 128, 1)
+                tail_low = pltpu.roll(tails, 128 - 16 * u, 1) if u else tails
                 tail_high = pltpu.roll(tails, (128 + REM - 16 * u) % 128, 1)
                 tail = jnp.where(
                     lane < REM,
@@ -370,7 +379,9 @@
                 strips = [unit[288:304, :].astype(F32), unit[304:320, :].astype(F32)]
                 strip = jnp.concatenate(
                     [
-                        pltpu.roll(strips[g // PER_ROW], (128 - STRIP * (g % PER_ROW)) % 128, 1)
+                        pltpu.roll(strips[g // PER_ROW], 128 - STRIP * (g % PER_ROW), 1)
+                        if g % PER_ROW
+                        else strips[g // PER_ROW]
                         for g in range(9)
                     ],
                     axis=0,
@@ -387,22 +398,19 @@
                 )
                 solved.append(y[:, 0:128])
                 wide = jnp.concatenate([y[:, 128:144], jnp.zeros((4 * PAIR_ROWS, 112), F32)], axis=1)
-                shifted_tail = pltpu.roll(wide, 16 * u, 1)
+                shifted_tail = pltpu.roll(wide, 16 * u, 1) if u else wide
                 keep = (lane >= 16 * u) & (lane < 16 * u + REM)
-                RA[...] += jnp.where(keep, shifted_tail, 0.0)
+                spread += jnp.where(keep, shifted_tail, 0.0)
             for k in range(4):
                 l = list_id(j, k // 2, k % 2)
                 part = slice(PAIR_ROWS * k, PAIR_ROWS * (k + 1))
                 (YR if k == 0 else YS)[l, rc, rows, :] = jnp.concatenate(
                     [solved[0][part], solved[1][part]], axis=0
                 ).astype(BF16)
-            return carry
-
-        lax.fori_loop(0, 4, body, 0)
         for k in range(4):
             l = list_id(j, k // 2, k % 2)
             part = jnp.concatenate(
-                [RA[PAIR_ROWS * k : PAIR_ROWS * (k + 1), :], jnp.zeros((MSG - CHUNK - PAIR_ROWS, 128), F32)], axis=0
+                [spread[PAIR_ROWS * k : PAIR_ROWS * (k + 1), :], jnp.zeros((MSG - CHUNK - PAIR_ROWS, 128), F32)], axis=0
             )
             (YR if k == 0 else YS)[l, rc, CHUNK:MSG, :] = part.astype(BF16)
             if k:
@@ -410,16 +418,22 @@
                 copy.start()
                 sent.append(copy)
 
-    for j in range(3):
-        pack(j, 1, 0)
-        pack(j, 1, 1)
-    send((1, 2, 0), (3, 2, 0), (1, 2, 1), (3, 2, 1))
+    pack(0, 1, 0)
+    pack(1, 1, 0)
+    pack(2, 1, 0)
+    pack(0, 1, 1)
+    pack(1, 1, 1)
+    pack(2, 1, 1)
+    send((1, 2, 0), (3, 2, 0))
     for j in range(3):
         pack(j, 0, 1)
-    send((2, 1, 0), (2, 1, 1), (2, 3, 0), (2, 3, 1))
+    send((1, 2, 1), (3, 2, 1))
+    fetch.wait()
     for j in range(3):
         pack(j, 0, 0)
         order_rows(j)
+    send((2, 1, 0), (2, 1, 1), (2, 3, 0), (2, 3, 1))
+    send((2, 2, 0), (2, 2, 1))
 
     got = set()
 
@@ -435,8 +449,9 @@
 
     for j in range(3):
         solve_ready(j, 0)
-    send((2, 2, 0), (2, 2, 1))
-    for rc in (1, 3, 2):
+    for j in range(3):
+        solve_ready(j, 1)
+    for rc in (3, 2):
         for j in range(3):
             solve_ready(j, rc)
     stores = []
@@ -455,7 +470,7 @@
         copy.wait_send()
 
 
-def exchange(inverses, state, drive, lows, held):
+def exchange(inverses, state, height, pressure, lows, held):
     any_space = pl.BlockSpec(memory_space=pl.ANY)
     smem = pl.BlockSpec(memory_space=pltpu.SMEM)
     messages = pltpu.VMEM((12, 4, MSG, 128), BF16)
@@ -465,15 +480,15 @@
             jax.ShapeDtypeStruct((12, 4, MSG, 128), BF16),
             jax.ShapeDtypeStruct((48, 128), jnp.int32),
         ),
-        in_specs=[any_space] * 3 + [smem, smem],
+        in_specs=[any_space] * 2 + [pl.BlockSpec(memory_space=pltpu.VMEM)] * 2 + [smem, smem],
         out_specs=(any_space, any_space),
         scratch_shapes=[
             pltpu.VMEM(inverses.shape, BF16),
             pltpu.VMEM(state.shape, BF16),
-            pltpu.VMEM(drive.shape, BF16),
+            pltpu.VMEM((144, 2 * LEV + 1), BF16),
             pltpu.VMEM((3, 4, 4, 2, UNIT, 128), BF16),
-            pltpu.VMEM((2, 4, 4, 4, 1, 128), jnp.int32),
-            pltpu.SMEM((2, 4, 4, 4, 1, 128), jnp.int32),
+            pltpu.VMEM((4, 4, 2, 4, 1, 128), jnp.int32),
+            pltpu.SMEM((4, 4, 2, 4, 1, 128), jnp.int32),
             pltpu.VMEM((48, 128), jnp.int32),
             pltpu.SMEM((48, 128), jnp.int32),
             pltpu.VMEM((ROWS, 128), F32),
@@ -482,15 +497,14 @@
             messages,
             messages,
             messages,
-            pltpu.VMEM((CHUNK, 128), F32),
-            pltpu.VMEM((CHUNK, 128), F32),
+            pltpu.VMEM((4, CHUNK, 128), F32),
+            pltpu.VMEM((4, CHUNK, 128), F32),
             pltpu.VMEM((3, 4 * PAIR_ROWS, 128), jnp.int32),
-            pltpu.VMEM((4 * PAIR_ROWS, 128), F32),
-            pltpu.SemaphoreType.DMA((6,)),
+            pltpu.SemaphoreType.DMA((5,)),
             pltpu.SemaphoreType.DMA((3, 4, 4, 2)),
             pltpu.SemaphoreType.DMA((3, 4, 4, 2)),
-            pltpu.SemaphoreType.DMA((10,)),
-            pltpu.SemaphoreType.DMA((10,)),
+            pltpu.SemaphoreType.DMA((13,)),
+            pltpu.SemaphoreType.DMA((13,)),
             pltpu.SemaphoreType.DMA((12,)),
             pltpu.SemaphoreType.DMA((12,)),
             pltpu.SemaphoreType.DMA((12, 4)),
@@ -500,31 +514,46 @@
         compiler_params=pltpu.CompilerParams(
             collective_id=0, has_side_effects=True, vmem_limit_bytes=60 * 1024 * 1024
         ),
-    )(inverses, state, drive, lows, held)
-
-
-def finish_kernel(yr, table, held, state, operator, out, YM, YT, TM, TR):
+    )(inverses, state, height, pressure, lows, held)
+
+
+def finish_kernel(yr, table, held, state, response, mass, out, OP, YM, YT, TM, TR):
     @pl.when(pl.program_id(0) == 0)
     def _():
-        def body(line, carry):
-            l, rc = line // 4, line % 4
-            TM[...] = yr[l, rc, 0:CHUNK, :].astype(F32)
-            tails = yr[l, rc, CHUNK:MSG, :].astype(F32)[0:PAIR_ROWS]
-            for u in range(8):
-                TR[PAIR_ROWS * u : PAIR_ROWS * (u + 1), :] = pltpu.roll(tails, 128 - 16 * u, 1) if u else tails
-            for u in range(8):
-                for to, of, put, row in copy_items(table, line, u, (YM, YT), (TM, TR)):
-                    to[pl.ds(row, 2), :] = of[put : put + 2, :]
+        def body(l, carry):
+            for rc in range(4):
+                TM[rc] = yr[l, rc, 0:CHUNK, :].astype(F32)
+                tails = yr[l, rc, CHUNK:MSG, :].astype(F32)[0:PAIR_ROWS]
+                for u in range(8):
+                    TR[rc, PAIR_ROWS * u : PAIR_ROWS * (u + 1), :] = pltpu.roll(tails, 128 - 16 * u, 1) if u else tails
+            for rc in range(4):
+                for u in range(8):
+                    for to, of, put, row in copy_items(table, 4 * l + rc, u, (YM, YT), (TM.at[rc], TR.at[rc])):
+                        to[pl.ds(row, 2), :] = of[put : put + 2, :]
             return carry
 
-        lax.fori_loop(0, 48, body, 0)
+        lax.fori_loop(0, 12, body, 0)
+        row = lax.broadcasted_iota(jnp.int32, OP.shape, 0)
+        col = lax.broadcasted_iota(jnp.int32, OP.shape, 1)
+        down = (
+            lax.broadcasted_iota(jnp.int32, (OP.shape[0], LEV), 0)
+            == lax.broadcasted_iota(jnp.int32, (OP.shape[0], LEV), 1) + LEV
+        ).astype(BF16)
+        across = (
+            lax.broadcasted_iota(jnp.int32, (LEV, 256), 0) == lax.broadcasted_iota(jnp.int32, (LEV, 256), 1)
+        ).astype(BF16)
+        wide = jnp.dot(response[...], across, preferred_element_type=F32).astype(BF16)
+        lower = jnp.dot(down, wide, preferred_element_type=F32)
+        masses = jnp.dot(jnp.broadcast_to(mass[...][None, :], (16, LEV)), across, preferred_element_type=F32)[0:1]
+        upper = jnp.where((row == col) & (col < LEV), 1.0, 0.0)
+        OP[...] = jnp.where(row < LEV, upper, jnp.where(row == 2 * LEV, -masses, -lower)).astype(BF16)
 
     rows = pl.ds(pl.multiple_of(pl.program_id(0) * TILE, TILE), TILE)
     nt = (((1,), (1,)), ((), ()))
     lanes = lax.broadcasted_iota(jnp.int32, (TILE, 128), 1)
     tail = jnp.where(lanes < REM, YT[rows, :], 0.0).astype(BF16)
-    total = lax.dot_general(operator[:, 0:128], YM[rows, :].astype(BF16), nt, preferred_element_type=F32)
-    total += lax.dot_general(operator[:, 128:256], tail, nt, preferred_element_type=F32)
+    columns = jnp.concatenate([YM[rows, :].astype(BF16), tail], axis=1)
+    total = lax.dot_general(OP[...], columns, nt, preferred_element_type=F32)[0 : 2 * LEV + 1]
     level = lax.broadcasted_iota(jnp.int32, total.shape, 0)
     total += jnp.where(level < LEV, 0.0, state[...].astype(F32))
     col = pl.program_id(0) * TILE + lax.broadcasted_iota(jnp.int32, (1, TILE), 1)
@@ -534,7 +563,7 @@
     out[...] = jnp.where(order >= 0, total, 0.0).astype(BF16)
 
 
-def finish(yr, table, held, state, operator):
+def finish(yr, table, held, state, response, mass):
     smem = pl.BlockSpec(memory_space=pltpu.SMEM)
     rows = state.shape[0]
     block = pl.BlockSpec((rows, TILE), lambda i: (0, i))
@@ -547,17 +576,19 @@
             smem,
             smem,
             block,
-            pl.BlockSpec((rows, 256), lambda i: (0, 0)),
+            pl.BlockSpec((LEV, LEV), lambda i: (0, 0)),
+            pl.BlockSpec((LEV,), lambda i: (0,)),
         ],
         out_specs=block,
         scratch_shapes=[
+            pltpu.VMEM((288, 256), BF16),
             pltpu.VMEM((TILE * TILES, 128), F32),
             pltpu.VMEM((TILE * TILES, 128), F32),
-            pltpu.VMEM((CHUNK, 128), F32),
-            pltpu.VMEM((CHUNK, 128), F32),
+            pltpu.VMEM((4, CHUNK, 128), F32),
+            pltpu.VMEM((4, CHUNK, 128), F32),
         ],
         compiler_params=pltpu.CompilerParams(vmem_limit_bytes=60 * 1024 * 1024),
-    )(yr, table, held, state, operator)
+    )(yr, table, held, state, response, mass)
 
 
 def shards(
@@ -570,13 +601,8 @@
     thermal_response_matrix,
     mass_row,
 ):
-    padded = jnp.pad(inverses, ((0, 0), (0, 0), (0, 144 - LEV), (0, 256 - LEV)))
-    drive = jnp.concatenate([jnp.zeros((LEV, LEV), BF16), height_operator, pressure_column[:, None]], axis=1)
-    drive = jnp.pad(drive, ((0, 144 - LEV), (0, 0)))
-    yr, table = exchange(padded, state, drive, pair_lows, held_orders)
-    operator = jnp.concatenate([jnp.eye(LEV, dtype=BF16), -thermal_response_matrix, -mass_row[None, :]], axis=0)
-    operator = jnp.pad(operator, ((0, 0), (0, 256 - LEV)))
-    return finish(yr, table, held_orders, state, operator)
+    yr, table = exchange(jnp.swapaxes(inverses, 1, 2), state, height_operator, pressure_column, pair_lows, held_orders)
+    return finish(yr, table, held_orders, state, thermal_response_matrix, mass_row)
 
 
 def solution(mesh):

time: 86.3 us -> 70 us (0.81)
  Pallas kernels: 79.3 us -> 69.7 us
  local copies, waits for them, and re-layouts: 3.31 us -> 0 us
  other arithmetic: 3.27 us -> 0 us
    pallas_call x1, Pallas kernels: 61.8 us -> 54.2 us  [exchange(): pl.pallas_call(exchange_kernel, out_shape=(jax.ShapeDtypeStruct((12, 4, M...]
    pallas_call x1, Pallas kernels: 17.4 us -> 15.6 us  [finish(): pl.pallas_call(finish_kernel, grid=(TILES,), out_shape=jax.ShapeDtypeStru...]
    concatenate x2 -> x0, other arithmetic: 1.7 us -> none  [the longest x1 0.99 us: shards(): jnp.concatenate([jnp.zeros((LEV, LEV), BF16), height_operator, pressure_c...]
    neg x2 -> x0, other arithmetic: 1.56 us -> none  [the longest x1 0.9 us: shards(): -thermal_response_matrix]
    pad x2 -> x0, local copies, waits for them, and re-layouts: 1.49 us -> none  [the longest x1 0.84 us: shards(): padded = jnp.pad(inverses, ((0, 0), (0, 0), (0, 144 - LEV), (0, 256 - LEV)))]
    unnamed x1 -> x0, local copies, waits for them, and re-layouts: 1.06 us -> none
where the time goes in v3:
time: 70 us; the launch traced here: 69.8 us
  Pallas kernels  69.7 us (100%)
    pallas_call x1, Pallas kernels, exchange(): pl.pallas_call(exchange_kernel, out_shape=(jax.ShapeDtypeStruct((12, 4, M...  54.2 us
    pallas_call x1, Pallas kernels, finish(): pl.pallas_call(finish_kernel, grid=(TILES,), out_shape=jax.ShapeDtypeStru...  15.6 us

profile of v3, /device:TPU:1, one launch (start us, length us, event | category | flops | bytes accessed | tf_op | source)
XLA Modules:
  0.0 69.8 jit_solution(12637986936173917290)
XLA Ops:
  0.0 54.2 %shard_map.82 = (bf16[12,4,224,128]{3,2,1,0:T(8,128)(2,1)}, s32[48,128]{1,0:T(8,128)}) custom-call(bf16[3,137,2,137]{3,2,1,0:T(2,128)(2,1)} %bitcast.1, bf16[275,7690]{1,0:T(8,128)(2,1)} %state.1, bf16[137,137]{1,0:T(8,128)(2,1)} %height.1, bf16[137]{0:T(256)(128)(2,1)} %pressure.1, s32[3]{0:T(128)} %lows.1, s32[5]{0:T(128)} %held.3), custom_call_target="tpu_custom_call" | custom-call | tf_op jit(solution)/shard_map/pallas_call | solution.py:477
  54.2 15.6 %shard_map.83 = bf16[275,7690]{1,0:T(8,128)(2,1)} custom-call(bf16[12,4,224,128]{3,2,1,0:T(8,128)(2,1)} %get-tuple-element.7.yr, s32[48,128]{1,0:T(8,128)} %get-tuple-element.8.table, s32[5]{0:T(128)} %held.3, bf16[275,7690]{1,0:T(8,128)(2,1)} %state.1, bf16[137,137]{1,0:T(8,128)(2,1)} %response.1, bf16[137]{0:T(256)(128)(2,1)} %mass.1), custom_call_target="tpu_custom_call" | custom-call | tf_op jit(solution)/shard_map/pallas_call | solution.py:570

commit v4 on v3

--- a/solution.py
+++ b/solution.py
@@ -30,8 +30,8 @@
 BLOCK = 768
 BLOCKS = 10
 TAIL_COLS = COLS - BLOCK * BLOCKS
-TILE = 1024
-TILES = 8
+TILE = 2048
+TILES = 4
 
 
 def list_id(j, t, e):

time: 70 us -> 68.1 us (0.973)
  Pallas kernels: 69.7 us -> 67.9 us
    pallas_call x1, Pallas kernels: 15.6 us -> 13.7 us  [finish(): pl.pallas_call(finish_kernel, grid=(TILES,), out_shape=jax.ShapeDtypeStru...]
where the time goes in v4:
time: 68.1 us; the launch traced here: 67.9 us
  Pallas kernels  67.9 us (100%)
    pallas_call x1, Pallas kernels, exchange(): pl.pallas_call(exchange_kernel, out_shape=(jax.ShapeDtypeStruct((12, 4, M...  54.2 us
    pallas_call x1, Pallas kernels, finish(): pl.pallas_call(finish_kernel, grid=(TILES,), out_shape=jax.ShapeDtypeStru...  13.7 us

profile of v4, /device:TPU:1, one launch (start us, length us, event | category | flops | bytes accessed | tf_op | source)
XLA Modules:
  0.0 67.9 jit_solution(10890500650517117376)
XLA Ops:
  0.0 54.2 %shard_map.82 = (bf16[12,4,224,128]{3,2,1,0:T(8,128)(2,1)}, s32[48,128]{1,0:T(8,128)}) custom-call(bf16[3,137,2,137]{3,2,1,0:T(2,128)(2,1)} %bitcast.1, bf16[275,7690]{1,0:T(8,128)(2,1)} %state.1, bf16[137,137]{1,0:T(8,128)(2,1)} %height.1, bf16[137]{0:T(256)(128)(2,1)} %pressure.1, s32[3]{0:T(128)} %lows.1, s32[5]{0:T(128)} %held.3), custom_call_target="tpu_custom_call" | custom-call | tf_op jit(solution)/shard_map/pallas_call | solution.py:477
  54.2 13.7 %shard_map.83 = bf16[275,7690]{1,0:T(8,128)(2,1)} custom-call(bf16[12,4,224,128]{3,2,1,0:T(8,128)(2,1)} %get-tuple-element.7.yr, s32[48,128]{1,0:T(8,128)} %get-tuple-element.8.table, s32[5]{0:T(128)} %held.3, bf16[275,7690]{1,0:T(8,128)(2,1)} %state.1, bf16[137,137]{1,0:T(8,128)(2,1)} %response.1, bf16[137]{0:T(256)(128)(2,1)} %mass.1), custom_call_target="tpu_custom_call" | custom-call | tf_op jit(solution)/shard_map/pallas_call | solution.py:570
